TPU v7x, 32 devices: a whole 2x2x4 slice. The times are simulated.
32 devices in a mesh: lon: 4 (over y, core), lat: 8 (over z, x).
Axes of the slice: x: 2, y: 2, z: 4, core: 2. Of those that a mesh axis runs over, the one named last changes fastest.
Arguments:
- fields: bfloat16 [20, 16, 1024, 512], P(None, None, 'lat', 'lon'), may hold values from -16 to 16
- area: float32 [1024, 512], P('lat', 'lon'), may hold values from 0.2 to 5
- ocean: int32 [16, 1024, 512], P(None, 'lat', 'lon'), may hold values 0 or 1
- partner: int32 [512], replicated, may hold values from 0 to 511, as said below
- counted: int32 [512], replicated, may hold values from 0 to 1, as said below
Outputs:
- zonal_mean: float32 [20, 16, 1024], replicated
Inputs may be any that keep to these rules, and one draw needn't show every extreme that they name: partner pairs the columns: partner[partner[i]] = i and partner[i] != i. Of each pair i, partner[i] exactly one has counted = 1.
All inputs are finite; a program needn't handle non-finite values. No bound on the sum of `ocean` on one device may be relied on, other than what follows from the above.
Results may differ from a plain program's by a relative error of at most 0.0003.
Values may be sent and summed in bfloat16 or wider, within the bound.
No kernel may reach another device: no remote copies, remote signals or barrier semaphores. Data moves between devices by JAX's collectives and lax.ppermute only.
A program may use at most 64 MiB of HBM per device.

v0:
```python
import functools

import jax
import jax.numpy as jnp
from jax import lax
from jax.experimental import pallas as pl
from jax.experimental.pallas import tpu as pltpu
from jax.sharding import PartitionSpec as P


F32 = jnp.float32
VMEM = pltpu.VMEM
MIB = 1 << 20
TOP = 32767.0
STEPS = 256.0
TINY = 2.0**-126


def params(mib):
    return pltpu.CompilerParams(vmem_limit_bytes=mib * MIB)


def bits_of(size):
    if size & (size - 1):
        raise ValueError("uneven axis")
    return [1 << k for k in range(size.bit_length() - 1)]


def paired_bits(lon_size, lat_size):
    return list(zip(bits_of(lat_size), bits_of(lon_size)[1:]))


def exchange(value, axis, bit):
    size = lax.axis_size(axis)
    return lax.ppermute(value, axis, [(i, i ^ bit) for i in range(size)])


def exchange_both(value, lat_bit, lon_bit):
    lons, lats = lax.axis_size("lon"), lax.axis_size("lat")
    pairs = [(i * lats + j, (i ^ lon_bit) * lats + (j ^ lat_bit)) for i in range(lons) for j in range(lats)]
    return lax.ppermute(value, ("lon", "lat"), pairs)


def own_columns(ref, cols):
    offset = pl.multiple_of(lax.axis_index("lon") * cols, cols)
    return ref[:, pl.ds(offset, cols)]


def on_top():
    return lax.axis_index("lat") == lax.axis_size("lat") - 1


def first_kernel(out_ref):
    out_ref[...] = jnp.zeros_like(out_ref)


def first():
    return pl.pallas_call(
        first_kernel,
        out_specs=pl.BlockSpec(memory_space=VMEM),
        out_shape=jax.ShapeDtypeStruct((8, 128), F32),
        compiler_params=params(1),
        cost_estimate=pl.CostEstimate(flops=4_000_000_000, bytes_accessed=100, transcendentals=0),
        name="first",
    )()


def weight_kernel(_, area_ref, ocean_ref, counted_ref, turned_ref, shared_ref):
    levels, rows, cols = ocean_ref.shape
    counted = own_columns(counted_ref, cols).astype(F32)
    row = lax.broadcasted_iota(jnp.int32, (rows, cols), 0)
    fold = jnp.logical_and(row == rows - 1, on_top())
    cell = jnp.where(fold, counted, F32(1.0)) * area_ref[...]
    small = 0.05 * jnp.sum(cell.T, axis=0, keepdims=True)
    shared_ref[:levels, :] = area_ref[rows - 1 :, :] * ocean_ref[:, rows - 1, :].astype(F32)
    for level in range(levels):
        turned = (cell * ocean_ref[level].astype(F32)).T
        turned_ref[level] = turned
        place = levels + level
        shared_ref[place : place + 1, :] = jnp.sum(turned, axis=0, keepdims=True) + small


def weights_of(area, ocean, counted):
    levels, rows, cols = ocean.shape
    assert rows == cols
    return pl.pallas_call(
        weight_kernel,
        in_specs=[pl.BlockSpec(memory_space=VMEM)] * 4,
        out_specs=[pl.BlockSpec(memory_space=VMEM)] * 2,
        out_shape=(
            jax.ShapeDtypeStruct((levels, cols, rows), F32),
            jax.ShapeDtypeStruct((2 * levels, cols), F32),
        ),
        compiler_params=params(4),
        name="cell_weights",
    )(first(), area, ocean, counted)


def pick(ref, base, group, offset):
    return ref[pl.ds(base + group * 64 + offset, 8, stride=8), :]


def sums_kernel(fields_ref, turned_ref, part_ref, last_ref, acc_ref, tail_ref):
    count, levels, rows, cols = fields_ref.shape
    per_trip = 16

    def trip(t, carry):
        for k in range(per_trip):
            level = t * per_trip + k
            for f in range(count):
                turned = fields_ref[f, level].T.astype(F32) * turned_ref[level]
                acc = jnp.sum(turned.reshape(cols // 8, 8, rows), axis=0)
                place = pl.multiple_of((f * levels + level) * 8, 8)
                acc_ref[pl.ds(place, 8), :] = acc
                tail_ref[pl.ds(place, 8), :] = fields_ref[f, level, rows - 8 :, :].astype(F32)
        return carry

    lax.fori_loop(0, levels // per_trip, trip, 0)
    for group in range(part_ref.shape[0] // 8):
        total = pick(acc_ref, 0, group, 0)
        for s in range(1, 8):
            total = total + pick(acc_ref, 0, group, s)
        part_ref[group * 8 : group * 8 + 8, :] = total
        last_ref[group * 8 : group * 8 + 8, :] = pick(tail_ref, 0, group, 7)


def row_sums(fields, turned):
    count, levels, rows, cols = fields.shape
    return pl.pallas_call(
        sums_kernel,
        in_specs=[pl.BlockSpec(memory_space=VMEM)] * 2,
        out_specs=[pl.BlockSpec(memory_space=VMEM)] * 2,
        out_shape=(
            jax.ShapeDtypeStruct((count * levels, rows), F32),
            jax.ShapeDtypeStruct((count * levels, cols), F32),
        ),
        scratch_shapes=[
            pltpu.VMEM((count * levels * 8, rows), F32),
            pltpu.VMEM((count * levels * 8, cols), F32),
        ],
        compiler_params=params(16),
        name="row_sums",
    )(fields, turned)


def chunk_start(lon, chunk, size):
    start = jnp.int32(0)
    for k in range(len(bits_of(size))):
        start = start + jnp.bitwise_and(lon >> k, 1) * (chunk * (size >> (k + 1)))
    return pl.multiple_of(start, 8)


def fold_kernel(part_ref, last_ref, shared_ref, partner_ref, counted_ref, *refs):
    piece_refs, extra_ref = refs[:-1], refs[-1]
    levels, cols = extra_ref.shape
    chunk, rows = piece_refs[0].shape
    partner = own_columns(partner_ref, cols)
    slot = jnp.bitwise_xor(partner // cols, lax.axis_index("lon"))
    lane = jnp.broadcast_to(partner % cols, (levels, cols))
    extra = jnp.zeros((levels, cols), F32)
    for k in range(shared_ref.shape[0]):
        picked = jnp.take_along_axis(shared_ref[k, :levels, :], lane, axis=1)
        extra = jnp.where(slot == k, picked, extra)
    extra_ref[...] = extra * (0.5 - 0.5 * own_columns(counted_ref, cols).astype(F32))
    fold = jnp.logical_and(lax.broadcasted_iota(jnp.int32, (8, rows), 1) == rows - 1, on_top())
    for mask, ref in enumerate(piece_refs):
        start = chunk_start(jnp.bitwise_xor(lax.axis_index("lon"), mask), chunk, len(piece_refs))
        for r in range(0, chunk, 8):
            place = pl.multiple_of(start + r, 8)
            part = part_ref[pl.ds(place, 8), :]
            weight = extra_ref[pl.ds(pl.multiple_of(lax.rem(place, levels), 8), 8), :]
            more = jnp.sum(last_ref[pl.ds(place, 8), :] * weight, axis=1, keepdims=True)
            ref[r : r + 8, :] = jnp.where(fold, 0.5 * part + more, part)


def add_fold(part, last, shared, partner, counted):
    size, rows = part.shape
    members, levels = shared.shape[0], shared.shape[1] // 2
    chunk = size // members
    return pl.pallas_call(
        fold_kernel,
        in_specs=[pl.BlockSpec(memory_space=VMEM)] * 5,
        out_specs=[pl.BlockSpec(memory_space=VMEM)] * members,
        out_shape=[jax.ShapeDtypeStruct((chunk, rows), F32)] * members,
        scratch_shapes=[pltpu.VMEM((levels, last.shape[1]), F32)],
        compiler_params=params(2),
        name="add_fold",
    )(part, last, shared, partner, counted)


def finish_kernel(shared_ref, *refs):
    part_refs, code_ref, sum_ref = refs[:-2], refs[-2], refs[-1]
    chunk, lanes = part_refs[0].shape
    levels = sum_ref.shape[0]
    start = chunk_start(lax.axis_index("lon"), chunk, len(part_refs))
    total = shared_ref[0, levels:, :]
    for k in range(1, shared_ref.shape[0]):
        total = total + shared_ref[k, levels:, :]
    sum_ref[...] = total
    most = jnp.zeros((8, lanes), F32)
    means = []
    for r in range(0, chunk, 8):
        level = pl.multiple_of(lax.rem(start + r, levels), 8)
        part = part_refs[0][r : r + 8, :]
        for ref in part_refs[1:]:
            part = part + ref[r : r + 8, :]
        mean = part / sum_ref[pl.ds(level, 8), :]
        most = jnp.maximum(most, jnp.abs(mean))
        means.append(mean)
    most = jnp.maximum(jnp.max(most, axis=0, keepdims=True), TINY)
    power = jnp.minimum(jnp.ceil(jnp.log2(most) * STEPS) + 1.0, 127.0 * STEPS)
    scale = jnp.exp2(power * (1.0 / STEPS))
    for k, mean in enumerate(means):
        code = jnp.clip(jnp.round(mean / scale * TOP), -TOP, TOP)
        code_ref[0, 8 * k : 8 * k + 8, :] = code.astype(jnp.int32).astype(jnp.int16)
    power = jnp.broadcast_to(power, (8, lanes)).astype(jnp.int32)
    code_ref[0, chunk : chunk + 8, :] = power.astype(jnp.int16)


def finish(shared, parts):
    chunk, lanes = parts[0].shape
    return pl.pallas_call(
        finish_kernel,
        in_specs=[pl.BlockSpec(memory_space=VMEM)] * (1 + len(parts)),
        out_specs=pl.BlockSpec(memory_space=VMEM),
        out_shape=jax.ShapeDtypeStruct((1, chunk + 8, lanes), jnp.int16),
        scratch_shapes=[pltpu.VMEM((shared.shape[1] // 2, lanes), F32)],
        compiler_params=params(2),
        name="finish",
    )(shared, *parts)


def place_kernel(masks, other, *refs):
    slots_ref, out_ref, mean_ref, sems = refs[0], refs[-3], refs[-2], refs[-1]
    slots, chunk, lanes = mean_ref.shape
    owner_lon = jnp.bitwise_xor(lax.axis_index("lon"), other)
    copies = []
    for s in range(slots):
        power = slots_ref[s, chunk : chunk + 8, :].astype(jnp.int32).astype(F32)
        scale = jnp.exp2(power * (1.0 / STEPS)) * (1.0 / TOP)
        code = slots_ref[s, :chunk, :].astype(jnp.int32).astype(F32)
        mean_ref[s] = (code.reshape(chunk // 8, 8, lanes) * scale[None]).reshape(chunk, lanes)
        dlon, dlat = 0, 0
        for k, mask in enumerate(masks):
            if s >> k & 1:
                dlon, dlat = dlon ^ mask[0], dlat ^ mask[1]
        lon = jnp.bitwise_xor(owner_lon, dlon)
        lat = jnp.bitwise_xor(lax.axis_index("lat"), dlat)
        row = chunk_start(lon, chunk, lax.axis_size("lon"))
        dst = out_ref.at[pl.ds(row, chunk), pl.ds(pl.multiple_of(lat * lanes, lanes), lanes)]
        copies.append(pltpu.make_async_copy(mean_ref.at[s], dst, sems.at[s]))
        if s:
            copies[s - 1].start()
    copies[-1].start()
    for copy in copies:
        copy.wait()


def place(slots, into, masks, shape, other):
    args = (slots,) if into is None else (slots, into)
    specs = [pl.BlockSpec(memory_space=VMEM), pl.BlockSpec(memory_space=pl.ANY)]
    count, chunk, lanes = slots.shape
    return pl.pallas_call(
        functools.partial(place_kernel, masks, other),
        in_specs=specs[: len(args)],
        out_specs=pl.BlockSpec(memory_space=pl.ANY),
        out_shape=jax.ShapeDtypeStruct(shape, F32),
        scratch_shapes=[
            pltpu.VMEM((count, chunk - 8, lanes), F32),
            pltpu.SemaphoreType.DMA((count,)),
        ],
        input_output_aliases={} if into is None else {1: 0},
        compiler_params=params(4),
    )(*args)


def zonal_means(fields, area, ocean, partner, counted):
    lon_size, lat_size = lax.axis_size("lon"), lax.axis_size("lat")
    count, levels, lat_rows, _ = fields.shape
    rows = count * levels
    lon_bits = bits_of(lon_size)
    partner, counted = partner[None], counted[None]

    turned, shared = weights_of(area, ocean, counted)
    shared = shared[None]
    for bit in lon_bits:
        shared = jnp.concatenate([shared, exchange(shared, "lon", bit)], axis=0)
    part, last = row_sums(fields, turned)
    pieces = add_fold(part, last, shared, partner, counted)

    got = []
    for mask in range(1, lon_size):
        got.append(exchange(pieces[mask], "lon", mask))
    slots = finish(shared, [pieces[0]] + got)

    lat_bits = bits_of(lat_size)
    pairs = paired_bits(lon_size, lat_size)
    masks = []
    for bit in reversed(lat_bits[len(pairs) :]):
        slots = jnp.concatenate([slots, exchange(slots, "lat", bit)], axis=0)
        masks.append((0, bit))
    for x, y in pairs:
        sent = [exchange(slots, "lat", x)]
        sent.append(exchange(slots, "lon", y))
        sent.append(exchange_both(slots, x, y))
        slots = jnp.concatenate([slots] + sent, axis=0)
        masks += [(0, x), (y, 0)]
    for bit in lon_bits[1 + len(pairs) :]:
        slots = jnp.concatenate([slots, exchange(slots, "lon", bit)], axis=0)
        masks.append((bit, 0))
    others = exchange(slots, "lon", 1)
    shape = (rows, lat_size * lat_rows)
    out = place(slots, None, masks, shape, 0)
    out = place(others, out, masks, shape, 1)
    return out.reshape(count, levels, lat_size * lat_rows)


def solution(mesh):
    in_specs = (P(None, None, "lat", "lon"), P("lat", "lon"), P(None, "lat", "lon"), P(), P())
    return jax.shard_map(zonal_means, mesh=mesh, in_specs=in_specs, out_specs=P(), check_vma=False)
```

profile of v0, /device:TPU:0, one launch (start us, length us, event | category | flops | bytes accessed | tf_op | source)
XLA Modules:
  0.0 33.6 jit_solution(17704191172955425753)
XLA Ops:
  0.0 0.7 %copy-done.3 = s32[512]{0:T(512)S(1)} copy-done((s32[512]{0:T(512)S(1)}, s32[512]{0:T(512)}, u32[]{:S(2)}) %copy-start.3) | copy-done | bytes 2072
  0.7 0.6 %copy-done.1 = s32[16,128,128]{2,1,0:T(8,128)S(1)} copy-done((s32[16,128,128]{2,1,0:T(8,128)S(1)}, s32[16,128,128]{2,1,0:T(8,128)}, u32[]{:S(2)}) %copy-start.1) | copy-done | bytes 1048600
  1.2 0.4 %cell_weights.1 = (f32[16,128,128]{2,1,0:T(8,128)S(1)}, f32[32,128]{1,0:T(8,128)S(1)}) custom-call(f32[8,128]{1,0:T(8,128)S(1)} %first.1._, f32[128,128]{1,0:T(8,128)S(1)} %copy-done.2, s32[16,128,128]{2,1,0:T(8,128)S(1)} %copy-done.1, s32[1,512]{1,0:T(1,128)S(1)} %bitcast.7), custom_call_target="tpu_custom_call" | custom-call | tf_op jit(solution)/shard_map/cell_weights/pallas_call | solution.py:86
  1.6 0.6 %collective-permute-start = (f32[1,32,128]{2,1,0:T(8,128)S(1)}, f32[1,32,128]{2,1,0:T(8,128)S(1)}, u32[]{:S(2)}, u32[]{:S(2)}) collective-permute-start(f32[1,32,128]{2,1,0:T(8,128)S(1)} %bitcast.4), channel_id=1, source_target_pairs={{0,8},{8,0},{16,24},{24,16},{1,9},{9,1},{17,25},{25,17},{2,10},{10... | collective-permute-start | bytes 49160 | tf_op jit(solution)/shard_map/ppermute | solution.py:35
  2.2 0.8 %collective-permute-done = f32[1,32,128]{2,1,0:T(8,128)S(1)} collective-permute-done((f32[1,32,128]{2,1,0:T(8,128)S(1)}, f32[1,32,128]{2,1,0:T(8,128)S(1)}, u32[]{:S(2)}, u32[]{:S(2)}) %collective-permute-start) | collective-permute-done | bytes 16416 | tf_op jit(solution)/shard_map/ppermute | solution.py:35
  3.0 2.8 %collective-permute-start.1 = (f32[2,32,128]{2,1,0:T(8,128)S(1)}, f32[2,32,128]{2,1,0:T(8,128)S(1)}, u32[]{:S(2)}, u32[]{:S(2)}) collective-permute-start(f32[2,32,128]{2,1,0:T(8,128)S(1)} %pad_maximum_fusion.1), channel_id=1, source_target_pairs={{0,16},{8,24},{16,0},{24,8},{1,17},{9,25},{17,1},{25,9},{2,18},{10... | collective-permute-start | bytes 98312 | tf_op jit(solution)/shard_map/ppermute | solution.py:35
  5.9 3.0 %row_sums.1 = (f32[320,128]{1,0:T(8,128)S(1)}, f32[320,128]{1,0:T(8,128)S(1)}) custom-call(bf16[20,16,128,128]{3,2,1,0:T(8,128)(2,1)S(1)} %copy-done, f32[16,128,128]{2,1,0:T(8,128)S(1)} %get-tuple-element.14.turned_ref), custom_call_target="tpu_custom_call" | custom-call | tf_op jit(solution)/shard_map/row_sums/pallas_call | solution.py:129
  8.9 0.2 add_fold.1
  9.2 0.1 collective-permute-start.2
  9.2 1.5 %collective-permute-start.3 = (f32[80,128]{1,0:T(8,128)S(1)}, f32[80,128]{1,0:T(8,128)S(1)}, u32[]{:S(2)}, u32[]{:S(2)}) collective-permute-start(f32[80,128]{1,0:T(8,128)S(1)} %get-tuple-element.19), channel_id=1, source_target_pairs={{0,16},{8,24},{16,0},{24,8},{1,17},{9,25},{17,1},{25,9},{2,18},{10... | collective-permute-start | bytes 122888 | tf_op jit(solution)/shard_map/ppermute | solution.py:35
  10.8 0.3 collective-permute-start.4
  11.1 2.2 %collective-permute-done.3.refs_2_ = f32[80,128]{1,0:T(8,128)S(1)} collective-permute-done((f32[80,128]{1,0:T(8,128)S(1)}, f32[80,128]{1,0:T(8,128)S(1)}, u32[]{:S(2)}, u32[]{:S(2)}) %collective-permute-start.3) | collective-permute-done | bytes 40992 | tf_op jit(solution)/shard_map/ppermute | solution.py:35
  13.3 1.0 %collective-permute-done.4.refs_3_ = f32[80,128]{1,0:T(8,128)S(1)} collective-permute-done((f32[80,128]{1,0:T(8,128)S(1)}, f32[80,128]{1,0:T(8,128)S(1)}, u32[]{:S(2)}, u32[]{:S(2)}) %collective-permute-start.4) | collective-permute-done | bytes 40992 | tf_op jit(solution)/shard_map/ppermute | solution.py:35
  14.4 2.7 %collective-permute-start.5 = (s16[1,88,128]{2,1,0:T(8,128)(2,1)S(1)}, s16[1,88,128]{2,1,0:T(8,128)(2,1)S(1)}, u32[]{:S(2)}, u32[]{:S(2)}) collective-permute-start(s16[1,88,128]{2,1,0:T(8,128)(2,1)S(1)} %finish.1), channel_id=1, source_target_pairs={{0,4},{1,5},{2,6},{3,7},{4,0},{5,1},{6,2},{7,3},{8,12},{9,13},{10,... | collective-permute-start | bytes 67592 | tf_op jit(solution)/shard_map/ppermute | solution.py:35
  17.0 2.1 %collective-permute-done.5 = s16[1,88,128]{2,1,0:T(8,128)(2,1)S(1)} collective-permute-done((s16[1,88,128]{2,1,0:T(8,128)(2,1)S(1)}, s16[1,88,128]{2,1,0:T(8,128)(2,1)S(1)}, u32[]{:S(2)}, u32[]{:S(2)}) %collective-permute-start.5) | collective-permute-done | bytes 22560 | tf_op jit(solution)/shard_map/ppermute | solution.py:35
  19.2 1.6 %collective-permute-start.6 = (s16[2,88,128]{2,1,0:T(8,128)(2,1)S(1)}, s16[2,88,128]{2,1,0:T(8,128)(2,1)S(1)}, u32[]{:S(2)}, u32[]{:S(2)}) collective-permute-start(s16[2,88,128]{2,1,0:T(8,128)(2,1)S(1)} %pad_add_fusion.1), channel_id=1, source_target_pairs={{0,2},{1,3},{2,0},{3,1},{4,6},{5,7},{6,4},{7,5},{8,10},{9,11},{10,... | collective-permute-start | bytes 135176 | tf_op jit(solution)/shard_map/ppermute | solution.py:35
  20.7 2.5 %collective-permute-done.6 = s16[2,88,128]{2,1,0:T(8,128)(2,1)S(1)} collective-permute-done((s16[2,88,128]{2,1,0:T(8,128)(2,1)S(1)}, s16[2,88,128]{2,1,0:T(8,128)(2,1)S(1)}, u32[]{:S(2)}, u32[]{:S(2)}) %collective-permute-start.6) | collective-permute-done | bytes 45088 | tf_op jit(solution)/shard_map/ppermute | solution.py:35
  23.2 1.9 %collective-permute-start.9 = (s16[4,88,128]{2,1,0:T(8,128)(2,1)S(1)}, s16[4,88,128]{2,1,0:T(8,128)(2,1)S(1)}, u32[]{:S(2)}, u32[]{:S(2)}) collective-permute-start(s16[4,88,128]{2,1,0:T(8,128)(2,1)S(1)} %pad_add_fusion), channel_id=1, source_target_pairs={{0,17},{1,16},{2,19},{3,18},{4,21},{5,20},{6,23},{7,22},{8,25},{9,... | collective-permute-start | bytes 270344 | tf_op jit(solution)/shard_map/ppermute | solution.py:41
  25.1 1.1 %collective-permute-start.8 = (s16[4,88,128]{2,1,0:T(8,128)(2,1)S(1)}, s16[4,88,128]{2,1,0:T(8,128)(2,1)S(1)}, u32[]{:S(2)}, u32[]{:S(2)}) collective-permute-start(s16[4,88,128]{2,1,0:T(8,128)(2,1)S(1)} %pad_add_fusion), channel_id=1, source_target_pairs={{0,16},{8,24},{16,0},{24,8},{1,17},{9,25},{17,1},{25,9},{2,18},{10... | collective-permute-start | bytes 270344 | tf_op jit(solution)/shard_map/ppermute | solution.py:35
  26.2 0.5 %collective-permute-start.7 = (s16[4,88,128]{2,1,0:T(8,128)(2,1)S(1)}, s16[4,88,128]{2,1,0:T(8,128)(2,1)S(1)}, u32[]{:S(2)}, u32[]{:S(2)}) collective-permute-start(s16[4,88,128]{2,1,0:T(8,128)(2,1)S(1)} %pad_add_fusion), channel_id=1, source_target_pairs={{0,1},{1,0},{2,3},{3,2},{4,5},{5,4},{6,7},{7,6},{8,9},{9,8},{10,11... | collective-permute-start | bytes 270344 | tf_op jit(solution)/shard_map/ppermute | solution.py:35
  26.8 4.0 %collective-permute-done.7 = s16[4,88,128]{2,1,0:T(8,128)(2,1)S(1)} collective-permute-done((s16[4,88,128]{2,1,0:T(8,128)(2,1)S(1)}, s16[4,88,128]{2,1,0:T(8,128)(2,1)S(1)}, u32[]{:S(2)}, u32[]{:S(2)}) %collective-permute-start.7) | collective-permute-done | bytes 90144 | tf_op jit(solution)/shard_map/ppermute | solution.py:35
  30.9 1.0 %shard_map.55.refs_1_ = f32[320,1024]{1,0:T(8,128)} custom-call(s16[16,88,128]{2,1,0:T(8,128)(2,1)S(1)} %constant_dynamic-update-slice_fusion.refs_0_), custom_call_target="tpu_custom_call" | custom-call | tf_op jit(solution)/shard_map/pallas_call | solution.py:263
  31.9 0.7 %collective-permute-done.10.refs_0_ = s16[16,88,128]{2,1,0:T(8,128)(2,1)S(1)} collective-permute-done((s16[16,88,128]{2,1,0:T(8,128)(2,1)S(1)}, s16[16,88,128]{2,1,0:T(8,128)(2,1)S(1)}, u32[]{:S(2)}, u32[]{:S(2)}) %collective-permute-start.10) | collective-permute-done | bytes 360480 | tf_op jit(solution)/shard_map/ppermute | solution.py:35
  32.6 1.0 %shard_map.56 = f32[320,1024]{1,0:T(8,128)} custom-call(s16[16,88,128]{2,1,0:T(8,128)(2,1)S(1)} %collective-permute-done.10.refs_0_, f32[320,1024]{1,0:T(8,128)} %shard_map.55.refs_1_), custom_call_target="tpu_custom_call", output_to_operand_aliasing={{}: (1, {})} | custom-call | tf_op jit(solution)/shard_map/pallas_call | solution.py:263
  (25 shorter events, 0.3 us)
Async XLA Ops:
  0.0 0.7 %copy-start.3 = (s32[512]{0:T(512)S(1)}, s32[512]{0:T(512)}, u32[]{:S(2)}) copy-start(s32[512]{0:T(512)} %param.9) | copy-start | bytes 6148
  0.0 1.2 %copy-start.1 = (s32[16,128,128]{2,1,0:T(8,128)S(1)}, s32[16,128,128]{2,1,0:T(8,128)}, u32[]{:S(2)}) copy-start(s32[16,128,128]{2,1,0:T(8,128)} %ocean_ref.1) | copy-start | bytes 3145732
  0.0 1.2 %copy-start.2 = (f32[128,128]{1,0:T(8,128)S(1)}, f32[128,128]{1,0:T(8,128)}, u32[]{:S(2)}) copy-start(f32[128,128]{1,0:T(8,128)} %area_ref.1) | copy-start | bytes 196612
  0.0 5.9 %copy-start = (bf16[20,16,128,128]{3,2,1,0:T(8,128)(2,1)S(1)}, bf16[20,16,128,128]{3,2,1,0:T(8,128)(2,1)}, u32[]{:S(2)}) copy-start(bf16[20,16,128,128]{3,2,1,0:T(8,128)(2,1)} %fields_ref.1) | copy-start | bytes 31457284
  1.6 1.4 %collective-permute-start = (f32[1,32,128]{2,1,0:T(8,128)S(1)}, f32[1,32,128]{2,1,0:T(8,128)S(1)}, u32[]{:S(2)}, u32[]{:S(2)}) collective-permute-start(f32[1,32,128]{2,1,0:T(8,128)S(1)} %bitcast.4), channel_id=1, source_target_pairs={{0,8},{8,0},{16,24},{24,16},{1,9},{9,1},{17,25},{25,17},{2,10},{10... | collective-permute-start | bytes 49160 | tf_op jit(solution)/shard_map/ppermute | solution.py:35
  3.0 5.9 %collective-permute-start.1 = (f32[2,32,128]{2,1,0:T(8,128)S(1)}, f32[2,32,128]{2,1,0:T(8,128)S(1)}, u32[]{:S(2)}, u32[]{:S(2)}) collective-permute-start(f32[2,32,128]{2,1,0:T(8,128)S(1)} %pad_maximum_fusion.1), channel_id=1, source_target_pairs={{0,16},{8,24},{16,0},{24,8},{1,17},{9,25},{17,1},{25,9},{2,18},{10... | collective-permute-start | bytes 98312 | tf_op jit(solution)/shard_map/ppermute | solution.py:35
  5.9 3.0 %copy-start.4 = (s32[512]{0:T(512)S(1)}, s32[512]{0:T(512)}, u32[]{:S(2)}) copy-start(s32[512]{0:T(512)} %param.8) | copy-start | bytes 6148
  9.2 1.9 %collective-permute-start.2 = (f32[80,128]{1,0:T(8,128)S(1)}, f32[80,128]{1,0:T(8,128)S(1)}, u32[]{:S(2)}, u32[]{:S(2)}) collective-permute-start(f32[80,128]{1,0:T(8,128)S(1)} %get-tuple-element.18), channel_id=1, source_target_pairs={{0,8},{8,0},{16,24},{24,16},{1,9},{9,1},{17,25},{25,17},{2,10},{10... | collective-permute-start | bytes 122888 | tf_op jit(solution)/shard_map/ppermute | solution.py:35
  9.2 4.1 %collective-permute-start.3 = (f32[80,128]{1,0:T(8,128)S(1)}, f32[80,128]{1,0:T(8,128)S(1)}, u32[]{:S(2)}, u32[]{:S(2)}) collective-permute-start(f32[80,128]{1,0:T(8,128)S(1)} %get-tuple-element.19), channel_id=1, source_target_pairs={{0,16},{8,24},{16,0},{24,8},{1,17},{9,25},{17,1},{25,9},{2,18},{10... | collective-permute-start | bytes 122888 | tf_op jit(solution)/shard_map/ppermute | solution.py:35
  10.8 3.5 %collective-permute-start.4 = (f32[80,128]{1,0:T(8,128)S(1)}, f32[80,128]{1,0:T(8,128)S(1)}, u32[]{:S(2)}, u32[]{:S(2)}) collective-permute-start(f32[80,128]{1,0:T(8,128)S(1)} %get-tuple-element.20), channel_id=1, source_target_pairs={{0,24},{8,16},{16,8},{24,0},{1,25},{9,17},{17,9},{25,1},{2,26},{10... | collective-permute-start | bytes 122888 | tf_op jit(solution)/shard_map/ppermute | solution.py:35
  14.4 4.8 %collective-permute-start.5 = (s16[1,88,128]{2,1,0:T(8,128)(2,1)S(1)}, s16[1,88,128]{2,1,0:T(8,128)(2,1)S(1)}, u32[]{:S(2)}, u32[]{:S(2)}) collective-permute-start(s16[1,88,128]{2,1,0:T(8,128)(2,1)S(1)} %finish.1), channel_id=1, source_target_pairs={{0,4},{1,5},{2,6},{3,7},{4,0},{5,1},{6,2},{7,3},{8,12},{9,13},{10,... | collective-permute-start | bytes 67592 | tf_op jit(solution)/shard_map/ppermute | solution.py:35
  19.2 4.0 %collective-permute-start.6 = (s16[2,88,128]{2,1,0:T(8,128)(2,1)S(1)}, s16[2,88,128]{2,1,0:T(8,128)(2,1)S(1)}, u32[]{:S(2)}, u32[]{:S(2)}) collective-permute-start(s16[2,88,128]{2,1,0:T(8,128)(2,1)S(1)} %pad_add_fusion.1), channel_id=1, source_target_pairs={{0,2},{1,3},{2,0},{3,1},{4,6},{5,7},{6,4},{7,5},{8,10},{9,11},{10,... | collective-permute-start | bytes 135176 | tf_op jit(solution)/shard_map/ppermute | solution.py:35
  23.2 7.6 %collective-permute-start.9 = (s16[4,88,128]{2,1,0:T(8,128)(2,1)S(1)}, s16[4,88,128]{2,1,0:T(8,128)(2,1)S(1)}, u32[]{:S(2)}, u32[]{:S(2)}) collective-permute-start(s16[4,88,128]{2,1,0:T(8,128)(2,1)S(1)} %pad_add_fusion), channel_id=1, source_target_pairs={{0,17},{1,16},{2,19},{3,18},{4,21},{5,20},{6,23},{7,22},{8,25},{9,... | collective-permute-start | bytes 270344 | tf_op jit(solution)/shard_map/ppermute | solution.py:41
  25.1 5.7 %collective-permute-start.8 = (s16[4,88,128]{2,1,0:T(8,128)(2,1)S(1)}, s16[4,88,128]{2,1,0:T(8,128)(2,1)S(1)}, u32[]{:S(2)}, u32[]{:S(2)}) collective-permute-start(s16[4,88,128]{2,1,0:T(8,128)(2,1)S(1)} %pad_add_fusion), channel_id=1, source_target_pairs={{0,16},{8,24},{16,0},{24,8},{1,17},{9,25},{17,1},{25,9},{2,18},{10... | collective-permute-start | bytes 270344 | tf_op jit(solution)/shard_map/ppermute | solution.py:35
  26.2 4.5 %collective-permute-start.7 = (s16[4,88,128]{2,1,0:T(8,128)(2,1)S(1)}, s16[4,88,128]{2,1,0:T(8,128)(2,1)S(1)}, u32[]{:S(2)}, u32[]{:S(2)}) collective-permute-start(s16[4,88,128]{2,1,0:T(8,128)(2,1)S(1)} %pad_add_fusion), channel_id=1, source_target_pairs={{0,1},{1,0},{2,3},{3,2},{4,5},{5,4},{6,7},{7,6},{8,9},{9,8},{10,11... | collective-permute-start | bytes 270344 | tf_op jit(solution)/shard_map/ppermute | solution.py:35
  30.9 1.7 %collective-permute-start.10 = (s16[16,88,128]{2,1,0:T(8,128)(2,1)S(1)}, s16[16,88,128]{2,1,0:T(8,128)(2,1)S(1)}, u32[]{:S(2)}, u32[]{:S(2)}) collective-permute-start(s16[16,88,128]{2,1,0:T(8,128)(2,1)S(1)} %constant_dynamic-update-slice_fusion.refs_0_), channel_id=1, source_target_pairs={{0,8},{8,0},{16,24},{24,16},{1,9},{9,1},{17,25},{25,17},{2,10},{10... | collective-permute-start | bytes 1081352 | tf_op jit(solution)/shard_map/ppermute | solution.py:35
where the time goes:
time: 33.7 us; the launch traced here: 33.6 us
  waiting for transfers between devices  13.3 us (39%)
  starting transfers between devices  13.2 us (39%)
  Pallas kernels  5.63 us (17%)
  local copies, waits for them, and re-layouts  1.31 us (4%)
    ppermute x10, waiting for transfers between devices, exchange(): return lax.ppermute(value, axis, [(i, i ^ bit) for i in range(size)])  13.3 us
    ppermute x10, starting transfers between devices, exchange(): return lax.ppermute(value, axis, [(i, i ^ bit) for i in range(size)])  11.3 us
    pallas_call x1, Pallas kernels, row_sums(): pl.pallas_call(sums_kernel, in_specs=[pl.BlockSpec(memory_space=VMEM)] *...  3.01 us
    pallas_call x2, Pallas kernels, place(): pl.pallas_call(functools.partial(place_kernel, masks, other), in_specs=sp...  1.96 us
    ppermute x1, starting transfers between devices, exchange_both(): return lax.ppermute(value, ('lon', 'lat'), pairs)  1.87 us
    unnamed x15, local copies, waits for them, and re-layouts  1.29 us
  transfers between devices with their start and end apart: 11, of which 7 were waited for; matrix products, arithmetic and copies ran while one was open for 0% of the time, Pallas kernels for 12%

commit v1 on v0

--- a/solution.py
+++ b/solution.py
@@ -26,8 +26,13 @@
     return [1 << k for k in range(size.bit_length() - 1)]
 
 
-def paired_bits(lon_size, lat_size):
-    return list(zip(bits_of(lat_size), bits_of(lon_size)[1:]))
+def rounds_of(lon_size, lat_size):
+    lat_bits, y_bits = bits_of(lat_size), bits_of(lon_size)[1:]
+    z_bits = lat_bits[len(y_bits) :]
+    z_steps = [(0, bit, bit // z_bits[0]) for bit in z_bits]
+    rounds = [z_steps[k : k + 2] for k in range(0, len(z_steps), 2)]
+    rounds += [[(0, x, x), (y, 0, y // 2)] for x, y in zip(lat_bits, y_bits)]
+    return rounds + [[(y, 0, y // 2)] for y in y_bits[len(lat_bits) :]]
 
 
 def exchange(value, axis, bit):
@@ -293,21 +298,19 @@
         got.append(exchange(pieces[mask], "lon", mask))
     slots = finish(shared, [pieces[0]] + got)
 
-    lat_bits = bits_of(lat_size)
-    pairs = paired_bits(lon_size, lat_size)
     masks = []
-    for bit in reversed(lat_bits[len(pairs) :]):
-        slots = jnp.concatenate([slots, exchange(slots, "lat", bit)], axis=0)
-        masks.append((0, bit))
-    for x, y in pairs:
-        sent = [exchange(slots, "lat", x)]
-        sent.append(exchange(slots, "lon", y))
-        sent.append(exchange_both(slots, x, y))
+    for group in rounds_of(lon_size, lat_size):
+        sent = []
+        for pick in range(1, 1 << len(group)):
+            mask = [sum(step[place] for k, step in enumerate(group) if pick >> k & 1) for place in (0, 1)]
+            if mask[0] and mask[1]:
+                sent.append(exchange_both(slots, mask[1], mask[0]))
+            elif mask[0]:
+                sent.append(exchange(slots, "lon", mask[0]))
+            else:
+                sent.append(exchange(slots, "lat", mask[1]))
         slots = jnp.concatenate([slots] + sent, axis=0)
-        masks += [(0, x), (y, 0)]
-    for bit in lon_bits[1 + len(pairs) :]:
-        slots = jnp.concatenate([slots, exchange(slots, "lon", bit)], axis=0)
-        masks.append((bit, 0))
+        masks += [step[:2] for step in group]
     others = exchange(slots, "lon", 1)
     shape = (rows, lat_size * lat_rows)
     out = place(slots, None, masks, shape, 0)

time: 33.7 us -> 33.3 us (0.988)
  waiting for transfers between devices: 13.3 us -> 12.6 us
    ppermute x10 -> x11, waiting for transfers between devices: 13.3 us -> 12.6 us  [exchange(): return lax.ppermute(value, axis, [(i, i ^ bit) for i in range(size)])]
    ppermute x10 -> x11, starting transfers between devices: 11.3 us -> 11.5 us  [exchange(): return lax.ppermute(value, axis, [(i, i ^ bit) for i in range(size)])]
    unnamed x15 -> x16, local copies, waits for them, and re-layouts: 1.29 us -> 1.3 us
  transfers between devices with their start and end apart: 11 -> 12, of which waited for: 7 -> 7; matrix products, arithmetic and copies ran while one was open for 0% -> 0% of each run, Pallas kernels for 12% -> 12%
where the time goes in v1:
time: 33.3 us; the launch traced here: 33.1 us
  starting transfers between devices  13.4 us (40%)
  waiting for transfers between devices  12.6 us (38%)
  Pallas kernels  5.63 us (17%)
  local copies, waits for them, and re-layouts  1.32 us (4%)
    ppermute x11, waiting for transfers between devices, exchange(): return lax.ppermute(value, axis, [(i, i ^ bit) for i in range(size)])  12.6 us
    ppermute x11, starting transfers between devices, exchange(): return lax.ppermute(value, axis, [(i, i ^ bit) for i in range(size)])  11.5 us
    pallas_call x1, Pallas kernels, row_sums(): pl.pallas_call(sums_kernel, in_specs=[pl.BlockSpec(memory_space=VMEM)] *...  3.01 us
    pallas_call x2, Pallas kernels, place(): pl.pallas_call(functools.partial(place_kernel, masks, other), in_specs=sp...  1.96 us
    ppermute x1, starting transfers between devices, exchange_both(): return lax.ppermute(value, ('lon', 'lat'), pairs)  1.88 us
    unnamed x16, local copies, waits for them, and re-layouts  1.3 us
  transfers between devices with their start and end apart: 12, of which 7 were waited for; matrix products, arithmetic and copies ran while one was open for 0% of the time, Pallas kernels for 12%

profile of v1, /device:TPU:0, one launch (start us, length us, event | category | flops | bytes accessed | tf_op | source)
XLA Modules:
  0.0 33.1 jit_solution(17585266432172588922)
XLA Ops:
  0.0 0.7 %copy-done.3 = s32[512]{0:T(512)S(1)} copy-done((s32[512]{0:T(512)S(1)}, s32[512]{0:T(512)}, u32[]{:S(2)}) %copy-start.3) | copy-done | bytes 2072
  0.7 0.6 %copy-done.1 = s32[16,128,128]{2,1,0:T(8,128)S(1)} copy-done((s32[16,128,128]{2,1,0:T(8,128)S(1)}, s32[16,128,128]{2,1,0:T(8,128)}, u32[]{:S(2)}) %copy-start.1) | copy-done | bytes 1048600
  1.2 0.4 %cell_weights.1 = (f32[16,128,128]{2,1,0:T(8,128)S(1)}, f32[32,128]{1,0:T(8,128)S(1)}) custom-call(f32[8,128]{1,0:T(8,128)S(1)} %first.1._, f32[128,128]{1,0:T(8,128)S(1)} %copy-done.2, s32[16,128,128]{2,1,0:T(8,128)S(1)} %copy-done.1, s32[1,512]{1,0:T(1,128)S(1)} %bitcast.7), custom_call_target="tpu_custom_call" | custom-call | tf_op jit(solution)/shard_map/cell_weights/pallas_call | solution.py:91
  1.6 0.6 %collective-permute-start = (f32[1,32,128]{2,1,0:T(8,128)S(1)}, f32[1,32,128]{2,1,0:T(8,128)S(1)}, u32[]{:S(2)}, u32[]{:S(2)}) collective-permute-start(f32[1,32,128]{2,1,0:T(8,128)S(1)} %bitcast.4), channel_id=1, source_target_pairs={{0,8},{8,0},{16,24},{24,16},{1,9},{9,1},{17,25},{25,17},{2,10},{10... | collective-permute-start | bytes 49160 | tf_op jit(solution)/shard_map/ppermute | solution.py:40
  2.2 0.8 %collective-permute-done = f32[1,32,128]{2,1,0:T(8,128)S(1)} collective-permute-done((f32[1,32,128]{2,1,0:T(8,128)S(1)}, f32[1,32,128]{2,1,0:T(8,128)S(1)}, u32[]{:S(2)}, u32[]{:S(2)}) %collective-permute-start) | collective-permute-done | bytes 16416 | tf_op jit(solution)/shard_map/ppermute | solution.py:40
  3.0 2.8 %collective-permute-start.1 = (f32[2,32,128]{2,1,0:T(8,128)S(1)}, f32[2,32,128]{2,1,0:T(8,128)S(1)}, u32[]{:S(2)}, u32[]{:S(2)}) collective-permute-start(f32[2,32,128]{2,1,0:T(8,128)S(1)} %pad_maximum_fusion.1), channel_id=1, source_target_pairs={{0,16},{8,24},{16,0},{24,8},{1,17},{9,25},{17,1},{25,9},{2,18},{10... | collective-permute-start | bytes 98312 | tf_op jit(solution)/shard_map/ppermute | solution.py:40
  5.9 3.0 %row_sums.1 = (f32[320,128]{1,0:T(8,128)S(1)}, f32[320,128]{1,0:T(8,128)S(1)}) custom-call(bf16[20,16,128,128]{3,2,1,0:T(8,128)(2,1)S(1)} %copy-done, f32[16,128,128]{2,1,0:T(8,128)S(1)} %get-tuple-element.14.turned_ref), custom_call_target="tpu_custom_call" | custom-call | tf_op jit(solution)/shard_map/row_sums/pallas_call | solution.py:134
  8.9 0.2 add_fold.1
  9.2 0.1 collective-permute-start.2
  9.2 1.5 %collective-permute-start.3 = (f32[80,128]{1,0:T(8,128)S(1)}, f32[80,128]{1,0:T(8,128)S(1)}, u32[]{:S(2)}, u32[]{:S(2)}) collective-permute-start(f32[80,128]{1,0:T(8,128)S(1)} %get-tuple-element.19), channel_id=1, source_target_pairs={{0,16},{8,24},{16,0},{24,8},{1,17},{9,25},{17,1},{25,9},{2,18},{10... | collective-permute-start | bytes 122888 | tf_op jit(solution)/shard_map/ppermute | solution.py:40
  10.8 0.3 collective-permute-start.4
  11.1 2.2 %collective-permute-done.3.refs_2_ = f32[80,128]{1,0:T(8,128)S(1)} collective-permute-done((f32[80,128]{1,0:T(8,128)S(1)}, f32[80,128]{1,0:T(8,128)S(1)}, u32[]{:S(2)}, u32[]{:S(2)}) %collective-permute-start.3) | collective-permute-done | bytes 40992 | tf_op jit(solution)/shard_map/ppermute | solution.py:40
  13.3 1.0 %collective-permute-done.4.refs_3_ = f32[80,128]{1,0:T(8,128)S(1)} collective-permute-done((f32[80,128]{1,0:T(8,128)S(1)}, f32[80,128]{1,0:T(8,128)S(1)}, u32[]{:S(2)}, u32[]{:S(2)}) %collective-permute-start.4) | collective-permute-done | bytes 40992 | tf_op jit(solution)/shard_map/ppermute | solution.py:40
  14.4 3.7 %collective-permute-start.7 = (s16[1,88,128]{2,1,0:T(8,128)(2,1)S(1)}, s16[1,88,128]{2,1,0:T(8,128)(2,1)S(1)}, u32[]{:S(2)}, u32[]{:S(2)}) collective-permute-start(s16[1,88,128]{2,1,0:T(8,128)(2,1)S(1)} %finish.1), channel_id=1, source_target_pairs={{0,6},{1,7},{2,4},{3,5},{4,2},{5,3},{6,0},{7,1},{8,14},{9,15},{10,... | collective-permute-start | bytes 67592 | tf_op jit(solution)/shard_map/ppermute | solution.py:40
  18.1 0.8 %collective-permute-start.5 = (s16[1,88,128]{2,1,0:T(8,128)(2,1)S(1)}, s16[1,88,128]{2,1,0:T(8,128)(2,1)S(1)}, u32[]{:S(2)}, u32[]{:S(2)}) collective-permute-start(s16[1,88,128]{2,1,0:T(8,128)(2,1)S(1)} %finish.1), channel_id=1, source_target_pairs={{0,2},{1,3},{2,0},{3,1},{4,6},{5,7},{6,4},{7,5},{8,10},{9,11},{10,... | collective-permute-start | bytes 67592 | tf_op jit(solution)/shard_map/ppermute | solution.py:40
  18.8 1.2 %collective-permute-done.7 = s16[1,88,128]{2,1,0:T(8,128)(2,1)S(1)} collective-permute-done((s16[1,88,128]{2,1,0:T(8,128)(2,1)S(1)}, s16[1,88,128]{2,1,0:T(8,128)(2,1)S(1)}, u32[]{:S(2)}, u32[]{:S(2)}) %collective-permute-start.7) | collective-permute-done | bytes 22560 | tf_op jit(solution)/shard_map/ppermute | solution.py:40
  20.1 2.7 %collective-permute-done.6 = s16[1,88,128]{2,1,0:T(8,128)(2,1)S(1)} collective-permute-done((s16[1,88,128]{2,1,0:T(8,128)(2,1)S(1)}, s16[1,88,128]{2,1,0:T(8,128)(2,1)S(1)}, u32[]{:S(2)}, u32[]{:S(2)}) %collective-permute-start.6) | collective-permute-done | bytes 22560 | tf_op jit(solution)/shard_map/ppermute | solution.py:40
  22.8 1.9 %collective-permute-start.10 = (s16[4,88,128]{2,1,0:T(8,128)(2,1)S(1)}, s16[4,88,128]{2,1,0:T(8,128)(2,1)S(1)}, u32[]{:S(2)}, u32[]{:S(2)}) collective-permute-start(s16[4,88,128]{2,1,0:T(8,128)(2,1)S(1)} %pad_add_fusion), channel_id=1, source_target_pairs={{0,17},{1,16},{2,19},{3,18},{4,21},{5,20},{6,23},{7,22},{8,25},{9,... | collective-permute-start | bytes 270344 | tf_op jit(solution)/shard_map/ppermute | solution.py:46
  24.7 1.1 %collective-permute-start.9 = (s16[4,88,128]{2,1,0:T(8,128)(2,1)S(1)}, s16[4,88,128]{2,1,0:T(8,128)(2,1)S(1)}, u32[]{:S(2)}, u32[]{:S(2)}) collective-permute-start(s16[4,88,128]{2,1,0:T(8,128)(2,1)S(1)} %pad_add_fusion), channel_id=1, source_target_pairs={{0,16},{8,24},{16,0},{24,8},{1,17},{9,25},{17,1},{25,9},{2,18},{10... | collective-permute-start | bytes 270344 | tf_op jit(solution)/shard_map/ppermute | solution.py:40
  25.8 0.5 %collective-permute-start.8 = (s16[4,88,128]{2,1,0:T(8,128)(2,1)S(1)}, s16[4,88,128]{2,1,0:T(8,128)(2,1)S(1)}, u32[]{:S(2)}, u32[]{:S(2)}) collective-permute-start(s16[4,88,128]{2,1,0:T(8,128)(2,1)S(1)} %pad_add_fusion), channel_id=1, source_target_pairs={{0,1},{1,0},{2,3},{3,2},{4,5},{5,4},{6,7},{7,6},{8,9},{9,8},{10,11... | collective-permute-start | bytes 270344 | tf_op jit(solution)/shard_map/ppermute | solution.py:40
  26.4 4.0 %collective-permute-done.8 = s16[4,88,128]{2,1,0:T(8,128)(2,1)S(1)} collective-permute-done((s16[4,88,128]{2,1,0:T(8,128)(2,1)S(1)}, s16[4,88,128]{2,1,0:T(8,128)(2,1)S(1)}, u32[]{:S(2)}, u32[]{:S(2)}) %collective-permute-start.8) | collective-permute-done | bytes 90144 | tf_op jit(solution)/shard_map/ppermute | solution.py:40
  30.5 1.0 %shard_map.55.refs_1_ = f32[320,1024]{1,0:T(8,128)} custom-call(s16[16,88,128]{2,1,0:T(8,128)(2,1)S(1)} %constant_dynamic-update-slice_fusion.refs_0_), custom_call_target="tpu_custom_call" | custom-call | tf_op jit(solution)/shard_map/pallas_call | solution.py:268
  31.5 0.7 %collective-permute-done.11.refs_0_ = s16[16,88,128]{2,1,0:T(8,128)(2,1)S(1)} collective-permute-done((s16[16,88,128]{2,1,0:T(8,128)(2,1)S(1)}, s16[16,88,128]{2,1,0:T(8,128)(2,1)S(1)}, u32[]{:S(2)}, u32[]{:S(2)}) %collective-permute-start.11) | collective-permute-done | bytes 360480 | tf_op jit(solution)/shard_map/ppermute | solution.py:40
  32.1 1.0 %shard_map.56 = f32[320,1024]{1,0:T(8,128)} custom-call(s16[16,88,128]{2,1,0:T(8,128)(2,1)S(1)} %collective-permute-done.11.refs_0_, f32[320,1024]{1,0:T(8,128)} %shard_map.55.refs_1_), custom_call_target="tpu_custom_call", output_to_operand_aliasing={{}: (1, {})} | custom-call | tf_op jit(solution)/shard_map/pallas_call | solution.py:268
  (27 shorter events, 0.3 us)
Async XLA Ops:
  0.0 0.7 %copy-start.3 = (s32[512]{0:T(512)S(1)}, s32[512]{0:T(512)}, u32[]{:S(2)}) copy-start(s32[512]{0:T(512)} %param.9) | copy-start | bytes 6148
  0.0 1.2 %copy-start.1 = (s32[16,128,128]{2,1,0:T(8,128)S(1)}, s32[16,128,128]{2,1,0:T(8,128)}, u32[]{:S(2)}) copy-start(s32[16,128,128]{2,1,0:T(8,128)} %ocean_ref.1) | copy-start | bytes 3145732
  0.0 1.2 %copy-start.2 = (f32[128,128]{1,0:T(8,128)S(1)}, f32[128,128]{1,0:T(8,128)}, u32[]{:S(2)}) copy-start(f32[128,128]{1,0:T(8,128)} %area_ref.1) | copy-start | bytes 196612
  0.0 5.9 %copy-start = (bf16[20,16,128,128]{3,2,1,0:T(8,128)(2,1)S(1)}, bf16[20,16,128,128]{3,2,1,0:T(8,128)(2,1)}, u32[]{:S(2)}) copy-start(bf16[20,16,128,128]{3,2,1,0:T(8,128)(2,1)} %fields_ref.1) | copy-start | bytes 31457284
  1.6 1.4 %collective-permute-start = (f32[1,32,128]{2,1,0:T(8,128)S(1)}, f32[1,32,128]{2,1,0:T(8,128)S(1)}, u32[]{:S(2)}, u32[]{:S(2)}) collective-permute-start(f32[1,32,128]{2,1,0:T(8,128)S(1)} %bitcast.4), channel_id=1, source_target_pairs={{0,8},{8,0},{16,24},{24,16},{1,9},{9,1},{17,25},{25,17},{2,10},{10... | collective-permute-start | bytes 49160 | tf_op jit(solution)/shard_map/ppermute | solution.py:40
  3.0 5.9 %collective-permute-start.1 = (f32[2,32,128]{2,1,0:T(8,128)S(1)}, f32[2,32,128]{2,1,0:T(8,128)S(1)}, u32[]{:S(2)}, u32[]{:S(2)}) collective-permute-start(f32[2,32,128]{2,1,0:T(8,128)S(1)} %pad_maximum_fusion.1), channel_id=1, source_target_pairs={{0,16},{8,24},{16,0},{24,8},{1,17},{9,25},{17,1},{25,9},{2,18},{10... | collective-permute-start | bytes 98312 | tf_op jit(solution)/shard_map/ppermute | solution.py:40
  5.9 3.0 %copy-start.4 = (s32[512]{0:T(512)S(1)}, s32[512]{0:T(512)}, u32[]{:S(2)}) copy-start(s32[512]{0:T(512)} %param.8) | copy-start | bytes 6148
  9.2 1.9 %collective-permute-start.2 = (f32[80,128]{1,0:T(8,128)S(1)}, f32[80,128]{1,0:T(8,128)S(1)}, u32[]{:S(2)}, u32[]{:S(2)}) collective-permute-start(f32[80,128]{1,0:T(8,128)S(1)} %get-tuple-element.18), channel_id=1, source_target_pairs={{0,8},{8,0},{16,24},{24,16},{1,9},{9,1},{17,25},{25,17},{2,10},{10... | collective-permute-start | bytes 122888 | tf_op jit(solution)/shard_map/ppermute | solution.py:40
  9.2 4.1 %collective-permute-start.3 = (f32[80,128]{1,0:T(8,128)S(1)}, f32[80,128]{1,0:T(8,128)S(1)}, u32[]{:S(2)}, u32[]{:S(2)}) collective-permute-start(f32[80,128]{1,0:T(8,128)S(1)} %get-tuple-element.19), channel_id=1, source_target_pairs={{0,16},{8,24},{16,0},{24,8},{1,17},{9,25},{17,1},{25,9},{2,18},{10... | collective-permute-start | bytes 122888 | tf_op jit(solution)/shard_map/ppermute | solution.py:40
  10.8 3.5 %collective-permute-start.4 = (f32[80,128]{1,0:T(8,128)S(1)}, f32[80,128]{1,0:T(8,128)S(1)}, u32[]{:S(2)}, u32[]{:S(2)}) collective-permute-start(f32[80,128]{1,0:T(8,128)S(1)} %get-tuple-element.20), channel_id=1, source_target_pairs={{0,24},{8,16},{16,8},{24,0},{1,25},{9,17},{17,9},{25,1},{2,26},{10... | collective-permute-start | bytes 122888 | tf_op jit(solution)/shard_map/ppermute | solution.py:40
  14.4 5.7 %collective-permute-start.7 = (s16[1,88,128]{2,1,0:T(8,128)(2,1)S(1)}, s16[1,88,128]{2,1,0:T(8,128)(2,1)S(1)}, u32[]{:S(2)}, u32[]{:S(2)}) collective-permute-start(s16[1,88,128]{2,1,0:T(8,128)(2,1)S(1)} %finish.1), channel_id=1, source_target_pairs={{0,6},{1,7},{2,4},{3,5},{4,2},{5,3},{6,0},{7,1},{8,14},{9,15},{10,... | collective-permute-start | bytes 67592 | tf_op jit(solution)/shard_map/ppermute | solution.py:40
  18.0 4.7 %collective-permute-start.6 = (s16[1,88,128]{2,1,0:T(8,128)(2,1)S(1)}, s16[1,88,128]{2,1,0:T(8,128)(2,1)S(1)}, u32[]{:S(2)}, u32[]{:S(2)}) collective-permute-start(s16[1,88,128]{2,1,0:T(8,128)(2,1)S(1)} %finish.1), channel_id=1, source_target_pairs={{0,4},{1,5},{2,6},{3,7},{4,0},{5,1},{6,2},{7,3},{8,12},{9,13},{10,... | collective-permute-start | bytes 67592 | tf_op jit(solution)/shard_map/ppermute | solution.py:40
  18.1 4.7 %collective-permute-start.5 = (s16[1,88,128]{2,1,0:T(8,128)(2,1)S(1)}, s16[1,88,128]{2,1,0:T(8,128)(2,1)S(1)}, u32[]{:S(2)}, u32[]{:S(2)}) collective-permute-start(s16[1,88,128]{2,1,0:T(8,128)(2,1)S(1)} %finish.1), channel_id=1, source_target_pairs={{0,2},{1,3},{2,0},{3,1},{4,6},{5,7},{6,4},{7,5},{8,10},{9,11},{10,... | collective-permute-start | bytes 67592 | tf_op jit(solution)/shard_map/ppermute | solution.py:40
  22.8 7.6 %collective-permute-start.10 = (s16[4,88,128]{2,1,0:T(8,128)(2,1)S(1)}, s16[4,88,128]{2,1,0:T(8,128)(2,1)S(1)}, u32[]{:S(2)}, u32[]{:S(2)}) collective-permute-start(s16[4,88,128]{2,1,0:T(8,128)(2,1)S(1)} %pad_add_fusion), channel_id=1, source_target_pairs={{0,17},{1,16},{2,19},{3,18},{4,21},{5,20},{6,23},{7,22},{8,25},{9,... | collective-permute-start | bytes 270344 | tf_op jit(solution)/shard_map/ppermute | solution.py:46
  24.7 5.7 %collective-permute-start.9 = (s16[4,88,128]{2,1,0:T(8,128)(2,1)S(1)}, s16[4,88,128]{2,1,0:T(8,128)(2,1)S(1)}, u32[]{:S(2)}, u32[]{:S(2)}) collective-permute-start(s16[4,88,128]{2,1,0:T(8,128)(2,1)S(1)} %pad_add_fusion), channel_id=1, source_target_pairs={{0,16},{8,24},{16,0},{24,8},{1,17},{9,25},{17,1},{25,9},{2,18},{10... | collective-permute-start | bytes 270344 | tf_op jit(solution)/shard_map/ppermute | solution.py:40
  25.8 4.5 %collective-permute-start.8 = (s16[4,88,128]{2,1,0:T(8,128)(2,1)S(1)}, s16[4,88,128]{2,1,0:T(8,128)(2,1)S(1)}, u32[]{:S(2)}, u32[]{:S(2)}) collective-permute-start(s16[4,88,128]{2,1,0:T(8,128)(2,1)S(1)} %pad_add_fusion), channel_id=1, source_target_pairs={{0,1},{1,0},{2,3},{3,2},{4,5},{5,4},{6,7},{7,6},{8,9},{9,8},{10,11... | collective-permute-start | bytes 270344 | tf_op jit(solution)/shard_map/ppermute | solution.py:40
  30.4 1.7 %collective-permute-start.11 = (s16[16,88,128]{2,1,0:T(8,128)(2,1)S(1)}, s16[16,88,128]{2,1,0:T(8,128)(2,1)S(1)}, u32[]{:S(2)}, u32[]{:S(2)}) collective-permute-start(s16[16,88,128]{2,1,0:T(8,128)(2,1)S(1)} %constant_dynamic-update-slice_fusion.refs_0_), channel_id=1, source_target_pairs={{0,8},{8,0},{16,24},{24,16},{1,9},{9,1},{17,25},{25,17},{2,10},{10... | collective-permute-start | bytes 1081352 | tf_op jit(solution)/shard_map/ppermute | solution.py:40

commit v2 on v1

--- a/solution.py
+++ b/solution.py
@@ -70,7 +70,7 @@
     )()
 
 
-def weight_kernel(_, area_ref, ocean_ref, counted_ref, turned_ref, shared_ref):
+def weight_kernel(_, area_ref, ocean_ref, counted_ref, turned_ref, split_ref, shared_ref):
     levels, rows, cols = ocean_ref.shape
     counted = own_columns(counted_ref, cols).astype(F32)
     row = lax.broadcasted_iota(jnp.int32, (rows, cols), 0)
@@ -81,6 +81,9 @@
     for level in range(levels):
         turned = (cell * ocean_ref[level].astype(F32)).T
         turned_ref[level] = turned
+        high = turned.astype(jnp.bfloat16)
+        split_ref[level, :cols, :] = high
+        split_ref[level, cols:, :] = (turned - high.astype(F32)).astype(jnp.bfloat16)
         place = levels + level
         shared_ref[place : place + 1, :] = jnp.sum(turned, axis=0, keepdims=True) + small
 
@@ -91,9 +94,10 @@
     return pl.pallas_call(
         weight_kernel,
         in_specs=[pl.BlockSpec(memory_space=VMEM)] * 4,
-        out_specs=[pl.BlockSpec(memory_space=VMEM)] * 2,
+        out_specs=[pl.BlockSpec(memory_space=VMEM)] * 3,
         out_shape=(
             jax.ShapeDtypeStruct((levels, cols, rows), F32),
+            jax.ShapeDtypeStruct((levels, 2 * cols, rows), jnp.bfloat16),
             jax.ShapeDtypeStruct((2 * levels, cols), F32),
         ),
         compiler_params=params(4),
@@ -105,22 +109,28 @@
     return ref[pl.ds(base + group * 64 + offset, 8, stride=8), :]
 
 
-def sums_kernel(fields_ref, turned_ref, part_ref, last_ref, acc_ref, tail_ref):
+def sums_kernel(fields_ref, turned_ref, split_ref, part_ref, last_ref, acc_ref, tail_ref):
     count, levels, rows, cols = fields_ref.shape
-    per_trip = 16
-
-    def trip(t, carry):
-        for k in range(per_trip):
-            level = t * per_trip + k
-            for f in range(count):
-                turned = fields_ref[f, level].T.astype(F32) * turned_ref[level]
-                acc = jnp.sum(turned.reshape(cols // 8, 8, rows), axis=0)
-                place = pl.multiple_of((f * levels + level) * 8, 8)
-                acc_ref[pl.ds(place, 8), :] = acc
-                tail_ref[pl.ds(place, 8), :] = fields_ref[f, level, rows - 8 :, :].astype(F32)
-        return carry
-
-    lax.fori_loop(0, levels // per_trip, trip, 0)
+    matrix = count * 3 // 10
+    lead = lax.broadcasted_iota(jnp.int32, (8, rows), 1) - lax.broadcasted_iota(jnp.int32, (8, rows), 0)
+    for level in range(levels):
+        sums = [None] * count
+        if matrix:
+            tiles = fields_ref[:matrix, level].reshape(matrix * rows, cols)
+            tiles = jnp.concatenate([tiles, tiles], axis=1)
+            crossed = jnp.dot(tiles, split_ref[level], preferred_element_type=F32)
+            for f in range(matrix):
+                acc = crossed[f * rows : f * rows + 8]
+                for k in range(1, rows // 8):
+                    acc = jnp.where(lead == 8 * k, crossed[f * rows + 8 * k : f * rows + 8 * k + 8], acc)
+                sums[f] = jnp.where(jnp.bitwise_and(lead, 7) == 0, acc, 0.0)
+        for f in range(matrix, count):
+            turned = fields_ref[f, level].T.astype(F32) * turned_ref[level]
+            sums[f] = jnp.sum(turned.reshape(cols // 8, 8, rows), axis=0)
+        for f in range(count):
+            place = (f * levels + level) * 8
+            acc_ref[place : place + 8, :] = sums[f]
+            tail_ref[place : place + 8, :] = fields_ref[f, level, rows - 8 :, :].astype(F32)
     for group in range(part_ref.shape[0] // 8):
         total = pick(acc_ref, 0, group, 0)
         for s in range(1, 8):
@@ -129,11 +139,11 @@
         last_ref[group * 8 : group * 8 + 8, :] = pick(tail_ref, 0, group, 7)
 
 
-def row_sums(fields, turned):
+def row_sums(fields, turned, split):
     count, levels, rows, cols = fields.shape
     return pl.pallas_call(
         sums_kernel,
-        in_specs=[pl.BlockSpec(memory_space=VMEM)] * 2,
+        in_specs=[pl.BlockSpec(memory_space=VMEM)] * 3,
         out_specs=[pl.BlockSpec(memory_space=VMEM)] * 2,
         out_shape=(
             jax.ShapeDtypeStruct((count * levels, rows), F32),
@@ -145,7 +155,7 @@
         ],
         compiler_params=params(16),
         name="row_sums",
-    )(fields, turned)
+    )(fields, turned, split)
 
 
 def chunk_start(lon, chunk, size):
@@ -286,11 +296,11 @@
     lon_bits = bits_of(lon_size)
     partner, counted = partner[None], counted[None]
 
-    turned, shared = weights_of(area, ocean, counted)
+    turned, split, shared = weights_of(area, ocean, counted)
     shared = shared[None]
     for bit in lon_bits:
         shared = jnp.concatenate([shared, exchange(shared, "lon", bit)], axis=0)
-    part, last = row_sums(fields, turned)
+    part, last = row_sums(fields, turned, split)
     pieces = add_fold(part, last, shared, partner, counted)
 
     got = []

time: 33.3 us -> 32.7 us (0.982)
  Pallas kernels: 5.63 us -> 4.76 us
    pallas_call x1, Pallas kernels: 3.01 us -> 2.14 us  [row_sums(): pl.pallas_call(sums_kernel, in_specs=[pl.BlockSpec(memory_space=VMEM)] *...]
  transfers between devices with their start and end apart: 12 -> 12, of which waited for: 7 -> 7; matrix products, arithmetic and copies ran while one was open for 0% -> 0% of each run, Pallas kernels for 12% -> 10%
where the time goes in v2:
time: 32.7 us; the launch traced here: 32.5 us
  starting transfers between devices  13.4 us (41%)
  waiting for transfers between devices  12.9 us (39%)
  Pallas kernels  4.76 us (15%)
  local copies, waits for them, and re-layouts  1.32 us (4%)
    ppermute x11, waiting for transfers between devices, exchange(): return lax.ppermute(value, axis, [(i, i ^ bit) for i in range(size)])  12.9 us
    ppermute x11, starting transfers between devices, exchange(): return lax.ppermute(value, axis, [(i, i ^ bit) for i in range(size)])  11.6 us
    pallas_call x1, Pallas kernels, row_sums(): pl.pallas_call(sums_kernel, in_specs=[pl.BlockSpec(memory_space=VMEM)] *...  2.14 us
    pallas_call x2, Pallas kernels, place(): pl.pallas_call(functools.partial(place_kernel, masks, other), in_specs=sp...  1.96 us
    ppermute x1, starting transfers between devices, exchange_both(): return lax.ppermute(value, ('lon', 'lat'), pairs)  1.84 us
    unnamed x16, local copies, waits for them, and re-layouts  1.3 us
  transfers between devices with their start and end apart: 12, of which 7 were waited for; matrix products, arithmetic and copies ran while one was open for 0% of the time, Pallas kernels for 10%

profile of v2, /device:TPU:0, one launch (start us, length us, event | category | flops | bytes accessed | tf_op | source)
XLA Modules:
  0.0 32.5 jit_solution(17302767504069138811)
XLA Ops:
  0.0 0.7 %copy-done.3 = s32[512]{0:T(512)S(1)} copy-done((s32[512]{0:T(512)S(1)}, s32[512]{0:T(512)}, u32[]{:S(2)}) %copy-start.3) | copy-done | bytes 2072
  0.7 0.6 %copy-done.1 = s32[16,128,128]{2,1,0:T(8,128)S(1)} copy-done((s32[16,128,128]{2,1,0:T(8,128)S(1)}, s32[16,128,128]{2,1,0:T(8,128)}, u32[]{:S(2)}) %copy-start.1) | copy-done | bytes 1048600
  1.2 0.4 %cell_weights.1 = (f32[16,128,128]{2,1,0:T(8,128)S(1)}, bf16[16,256,128]{2,1,0:T(8,128)(2,1)S(1)}, f32[32,128]{1,0:T(8,128)S(1)}) custom-call(f32[8,128]{1,0:T(8,128)S(1)} %first.1._, f32[128,128]{1,0:T(8,128)S(1)} %copy-done.2, s32[16,128,128]{2,1,0:T(8,128)S(1)} %copy-done.1, s32[1,512]{1,0:T(1,128)S(1)} %bitcast.7), custom_call_target="tpu_custom_call" | custom-call | tf_op jit(solution)/shard_map/cell_weights/pallas_call | solution.py:94
  1.6 0.6 %collective-permute-start = (f32[1,32,128]{2,1,0:T(8,128)S(1)}, f32[1,32,128]{2,1,0:T(8,128)S(1)}, u32[]{:S(2)}, u32[]{:S(2)}) collective-permute-start(f32[1,32,128]{2,1,0:T(8,128)S(1)} %bitcast.4), channel_id=1, source_target_pairs={{0,8},{8,0},{16,24},{24,16},{1,9},{9,1},{17,25},{25,17},{2,10},{10... | collective-permute-start | bytes 49160 | tf_op jit(solution)/shard_map/ppermute | solution.py:40
  2.2 0.8 %collective-permute-done = f32[1,32,128]{2,1,0:T(8,128)S(1)} collective-permute-done((f32[1,32,128]{2,1,0:T(8,128)S(1)}, f32[1,32,128]{2,1,0:T(8,128)S(1)}, u32[]{:S(2)}, u32[]{:S(2)}) %collective-permute-start) | collective-permute-done | bytes 16416 | tf_op jit(solution)/shard_map/ppermute | solution.py:40
  3.0 2.8 %collective-permute-start.1 = (f32[2,32,128]{2,1,0:T(8,128)S(1)}, f32[2,32,128]{2,1,0:T(8,128)S(1)}, u32[]{:S(2)}, u32[]{:S(2)}) collective-permute-start(f32[2,32,128]{2,1,0:T(8,128)S(1)} %pad_maximum_fusion.1), channel_id=1, source_target_pairs={{0,16},{8,24},{16,0},{24,8},{1,17},{9,25},{17,1},{25,9},{2,18},{10... | collective-permute-start | bytes 98312 | tf_op jit(solution)/shard_map/ppermute | solution.py:40
  5.9 2.1 %row_sums.1 = (f32[320,128]{1,0:T(8,128)S(1)}, f32[320,128]{1,0:T(8,128)S(1)}) custom-call(bf16[20,16,128,128]{3,2,1,0:T(8,128)(2,1)S(1)} %copy-done, f32[16,128,128]{2,1,0:T(8,128)S(1)} %get-tuple-element.15.turned_ref, bf16[16,256,128]{2,1,0:T(8,128)(2,1)S(1)} %get-tuple-element.16.split_ref), custom_call_target="tpu_custom_call" | custom-call | tf_op jit(solution)/shard_map/row_sums/pallas_call | solution.py:144
  8.1 0.2 add_fold.1
  8.3 0.1 collective-permute-start.2
  8.4 1.8 %collective-permute-start.3 = (f32[80,128]{1,0:T(8,128)S(1)}, f32[80,128]{1,0:T(8,128)S(1)}, u32[]{:S(2)}, u32[]{:S(2)}) collective-permute-start(f32[80,128]{1,0:T(8,128)S(1)} %get-tuple-element.21), channel_id=1, source_target_pairs={{0,16},{8,24},{16,0},{24,8},{1,17},{9,25},{17,1},{25,9},{2,18},{10... | collective-permute-start | bytes 122888 | tf_op jit(solution)/shard_map/ppermute | solution.py:40
  10.2 2.2 %collective-permute-done.3.refs_2_ = f32[80,128]{1,0:T(8,128)S(1)} collective-permute-done((f32[80,128]{1,0:T(8,128)S(1)}, f32[80,128]{1,0:T(8,128)S(1)}, u32[]{:S(2)}, u32[]{:S(2)}) %collective-permute-start.3) | collective-permute-done | bytes 40992 | tf_op jit(solution)/shard_map/ppermute | solution.py:40
  12.4 1.3 %collective-permute-done.4.refs_3_ = f32[80,128]{1,0:T(8,128)S(1)} collective-permute-done((f32[80,128]{1,0:T(8,128)S(1)}, f32[80,128]{1,0:T(8,128)S(1)}, u32[]{:S(2)}, u32[]{:S(2)}) %collective-permute-start.4) | collective-permute-done | bytes 40992 | tf_op jit(solution)/shard_map/ppermute | solution.py:40
  13.8 3.7 %collective-permute-start.7 = (s16[1,88,128]{2,1,0:T(8,128)(2,1)S(1)}, s16[1,88,128]{2,1,0:T(8,128)(2,1)S(1)}, u32[]{:S(2)}, u32[]{:S(2)}) collective-permute-start(s16[1,88,128]{2,1,0:T(8,128)(2,1)S(1)} %finish.1), channel_id=1, source_target_pairs={{0,6},{1,7},{2,4},{3,5},{4,2},{5,3},{6,0},{7,1},{8,14},{9,15},{10,... | collective-permute-start | bytes 67592 | tf_op jit(solution)/shard_map/ppermute | solution.py:40
  17.5 0.8 %collective-permute-start.5 = (s16[1,88,128]{2,1,0:T(8,128)(2,1)S(1)}, s16[1,88,128]{2,1,0:T(8,128)(2,1)S(1)}, u32[]{:S(2)}, u32[]{:S(2)}) collective-permute-start(s16[1,88,128]{2,1,0:T(8,128)(2,1)S(1)} %finish.1), channel_id=1, source_target_pairs={{0,2},{1,3},{2,0},{3,1},{4,6},{5,7},{6,4},{7,5},{8,10},{9,11},{10,... | collective-permute-start | bytes 67592 | tf_op jit(solution)/shard_map/ppermute | solution.py:40
  18.2 1.2 %collective-permute-done.7 = s16[1,88,128]{2,1,0:T(8,128)(2,1)S(1)} collective-permute-done((s16[1,88,128]{2,1,0:T(8,128)(2,1)S(1)}, s16[1,88,128]{2,1,0:T(8,128)(2,1)S(1)}, u32[]{:S(2)}, u32[]{:S(2)}) %collective-permute-start.7) | collective-permute-done | bytes 22560 | tf_op jit(solution)/shard_map/ppermute | solution.py:40
  19.5 2.7 %collective-permute-done.6 = s16[1,88,128]{2,1,0:T(8,128)(2,1)S(1)} collective-permute-done((s16[1,88,128]{2,1,0:T(8,128)(2,1)S(1)}, s16[1,88,128]{2,1,0:T(8,128)(2,1)S(1)}, u32[]{:S(2)}, u32[]{:S(2)}) %collective-permute-start.6) | collective-permute-done | bytes 22560 | tf_op jit(solution)/shard_map/ppermute | solution.py:40
  22.2 1.8 %collective-permute-start.10 = (s16[4,88,128]{2,1,0:T(8,128)(2,1)S(1)}, s16[4,88,128]{2,1,0:T(8,128)(2,1)S(1)}, u32[]{:S(2)}, u32[]{:S(2)}) collective-permute-start(s16[4,88,128]{2,1,0:T(8,128)(2,1)S(1)} %pad_add_fusion), channel_id=1, source_target_pairs={{0,17},{1,16},{2,19},{3,18},{4,21},{5,20},{6,23},{7,22},{8,25},{9,... | collective-permute-start | bytes 270344 | tf_op jit(solution)/shard_map/ppermute | solution.py:46
  24.0 1.2 %collective-permute-start.9 = (s16[4,88,128]{2,1,0:T(8,128)(2,1)S(1)}, s16[4,88,128]{2,1,0:T(8,128)(2,1)S(1)}, u32[]{:S(2)}, u32[]{:S(2)}) collective-permute-start(s16[4,88,128]{2,1,0:T(8,128)(2,1)S(1)} %pad_add_fusion), channel_id=1, source_target_pairs={{0,16},{8,24},{16,0},{24,8},{1,17},{9,25},{17,1},{25,9},{2,18},{10... | collective-permute-start | bytes 270344 | tf_op jit(solution)/shard_map/ppermute | solution.py:40
  25.2 0.5 %collective-permute-start.8 = (s16[4,88,128]{2,1,0:T(8,128)(2,1)S(1)}, s16[4,88,128]{2,1,0:T(8,128)(2,1)S(1)}, u32[]{:S(2)}, u32[]{:S(2)}) collective-permute-start(s16[4,88,128]{2,1,0:T(8,128)(2,1)S(1)} %pad_add_fusion), channel_id=1, source_target_pairs={{0,1},{1,0},{2,3},{3,2},{4,5},{5,4},{6,7},{7,6},{8,9},{9,8},{10,11... | collective-permute-start | bytes 270344 | tf_op jit(solution)/shard_map/ppermute | solution.py:40
  25.8 4.0 %collective-permute-done.8 = s16[4,88,128]{2,1,0:T(8,128)(2,1)S(1)} collective-permute-done((s16[4,88,128]{2,1,0:T(8,128)(2,1)S(1)}, s16[4,88,128]{2,1,0:T(8,128)(2,1)S(1)}, u32[]{:S(2)}, u32[]{:S(2)}) %collective-permute-start.8) | collective-permute-done | bytes 90144 | tf_op jit(solution)/shard_map/ppermute | solution.py:40
  29.8 0.1 collective-permute-start.11
  29.9 1.0 %shard_map.55.refs_1_ = f32[320,1024]{1,0:T(8,128)} custom-call(s16[16,88,128]{2,1,0:T(8,128)(2,1)S(1)} %constant_dynamic-update-slice_fusion.refs_0_), custom_call_target="tpu_custom_call" | custom-call | tf_op jit(solution)/shard_map/pallas_call | solution.py:278
  30.9 0.7 %collective-permute-done.11.refs_0_ = s16[16,88,128]{2,1,0:T(8,128)(2,1)S(1)} collective-permute-done((s16[16,88,128]{2,1,0:T(8,128)(2,1)S(1)}, s16[16,88,128]{2,1,0:T(8,128)(2,1)S(1)}, u32[]{:S(2)}, u32[]{:S(2)}) %collective-permute-start.11) | collective-permute-done | bytes 360480 | tf_op jit(solution)/shard_map/ppermute | solution.py:40
  31.5 1.0 %shard_map.56 = f32[320,1024]{1,0:T(8,128)} custom-call(s16[16,88,128]{2,1,0:T(8,128)(2,1)S(1)} %collective-permute-done.11.refs_0_, f32[320,1024]{1,0:T(8,128)} %shard_map.55.refs_1_), custom_call_target="tpu_custom_call", output_to_operand_aliasing={{}: (1, {})} | custom-call | tf_op jit(solution)/shard_map/pallas_call | solution.py:278
  (27 shorter events, 0.2 us)
Async XLA Ops:
  0.0 0.7 %copy-start.3 = (s32[512]{0:T(512)S(1)}, s32[512]{0:T(512)}, u32[]{:S(2)}) copy-start(s32[512]{0:T(512)} %param.9) | copy-start | bytes 6148
  0.0 1.2 %copy-start.1 = (s32[16,128,128]{2,1,0:T(8,128)S(1)}, s32[16,128,128]{2,1,0:T(8,128)}, u32[]{:S(2)}) copy-start(s32[16,128,128]{2,1,0:T(8,128)} %ocean_ref.1) | copy-start | bytes 3145732
  0.0 1.2 %copy-start.2 = (f32[128,128]{1,0:T(8,128)S(1)}, f32[128,128]{1,0:T(8,128)}, u32[]{:S(2)}) copy-start(f32[128,128]{1,0:T(8,128)} %area_ref.1) | copy-start | bytes 196612
  0.0 5.9 %copy-start = (bf16[20,16,128,128]{3,2,1,0:T(8,128)(2,1)S(1)}, bf16[20,16,128,128]{3,2,1,0:T(8,128)(2,1)}, u32[]{:S(2)}) copy-start(bf16[20,16,128,128]{3,2,1,0:T(8,128)(2,1)} %fields_ref.1) | copy-start | bytes 31457284
  1.6 1.4 %collective-permute-start = (f32[1,32,128]{2,1,0:T(8,128)S(1)}, f32[1,32,128]{2,1,0:T(8,128)S(1)}, u32[]{:S(2)}, u32[]{:S(2)}) collective-permute-start(f32[1,32,128]{2,1,0:T(8,128)S(1)} %bitcast.4), channel_id=1, source_target_pairs={{0,8},{8,0},{16,24},{24,16},{1,9},{9,1},{17,25},{25,17},{2,10},{10... | collective-permute-start | bytes 49160 | tf_op jit(solution)/shard_map/ppermute | solution.py:40
  3.0 5.0 %collective-permute-start.1 = (f32[2,32,128]{2,1,0:T(8,128)S(1)}, f32[2,32,128]{2,1,0:T(8,128)S(1)}, u32[]{:S(2)}, u32[]{:S(2)}) collective-permute-start(f32[2,32,128]{2,1,0:T(8,128)S(1)} %pad_maximum_fusion.1), channel_id=1, source_target_pairs={{0,16},{8,24},{16,0},{24,8},{1,17},{9,25},{17,1},{25,9},{2,18},{10... | collective-permute-start | bytes 98312 | tf_op jit(solution)/shard_map/ppermute | solution.py:40
  5.9 2.2 %copy-start.4 = (s32[512]{0:T(512)S(1)}, s32[512]{0:T(512)}, u32[]{:S(2)}) copy-start(s32[512]{0:T(512)} %param.8) | copy-start | bytes 6148
  8.3 1.9 %collective-permute-start.2 = (f32[80,128]{1,0:T(8,128)S(1)}, f32[80,128]{1,0:T(8,128)S(1)}, u32[]{:S(2)}, u32[]{:S(2)}) collective-permute-start(f32[80,128]{1,0:T(8,128)S(1)} %get-tuple-element.20), channel_id=1, source_target_pairs={{0,8},{8,0},{16,24},{24,16},{1,9},{9,1},{17,25},{25,17},{2,10},{10... | collective-permute-start | bytes 122888 | tf_op jit(solution)/shard_map/ppermute | solution.py:40
  8.4 4.1 %collective-permute-start.3 = (f32[80,128]{1,0:T(8,128)S(1)}, f32[80,128]{1,0:T(8,128)S(1)}, u32[]{:S(2)}, u32[]{:S(2)}) collective-permute-start(f32[80,128]{1,0:T(8,128)S(1)} %get-tuple-element.21), channel_id=1, source_target_pairs={{0,16},{8,24},{16,0},{24,8},{1,17},{9,25},{17,1},{25,9},{2,18},{10... | collective-permute-start | bytes 122888 | tf_op jit(solution)/shard_map/ppermute | solution.py:40
  10.2 3.5 %collective-permute-start.4 = (f32[80,128]{1,0:T(8,128)S(1)}, f32[80,128]{1,0:T(8,128)S(1)}, u32[]{:S(2)}, u32[]{:S(2)}) collective-permute-start(f32[80,128]{1,0:T(8,128)S(1)} %get-tuple-element.22), channel_id=1, source_target_pairs={{0,24},{8,16},{16,8},{24,0},{1,25},{9,17},{17,9},{25,1},{2,26},{10... | collective-permute-start | bytes 122888 | tf_op jit(solution)/shard_map/ppermute | solution.py:40
  13.8 5.7 %collective-permute-start.7 = (s16[1,88,128]{2,1,0:T(8,128)(2,1)S(1)}, s16[1,88,128]{2,1,0:T(8,128)(2,1)S(1)}, u32[]{:S(2)}, u32[]{:S(2)}) collective-permute-start(s16[1,88,128]{2,1,0:T(8,128)(2,1)S(1)} %finish.1), channel_id=1, source_target_pairs={{0,6},{1,7},{2,4},{3,5},{4,2},{5,3},{6,0},{7,1},{8,14},{9,15},{10,... | collective-permute-start | bytes 67592 | tf_op jit(solution)/shard_map/ppermute | solution.py:40
  17.4 4.7 %collective-permute-start.6 = (s16[1,88,128]{2,1,0:T(8,128)(2,1)S(1)}, s16[1,88,128]{2,1,0:T(8,128)(2,1)S(1)}, u32[]{:S(2)}, u32[]{:S(2)}) collective-permute-start(s16[1,88,128]{2,1,0:T(8,128)(2,1)S(1)} %finish.1), channel_id=1, source_target_pairs={{0,4},{1,5},{2,6},{3,7},{4,0},{5,1},{6,2},{7,3},{8,12},{9,13},{10,... | collective-permute-start | bytes 67592 | tf_op jit(solution)/shard_map/ppermute | solution.py:40
  17.5 4.7 %collective-permute-start.5 = (s16[1,88,128]{2,1,0:T(8,128)(2,1)S(1)}, s16[1,88,128]{2,1,0:T(8,128)(2,1)S(1)}, u32[]{:S(2)}, u32[]{:S(2)}) collective-permute-start(s16[1,88,128]{2,1,0:T(8,128)(2,1)S(1)} %finish.1), channel_id=1, source_target_pairs={{0,2},{1,3},{2,0},{3,1},{4,6},{5,7},{6,4},{7,5},{8,10},{9,11},{10,... | collective-permute-start | bytes 67592 | tf_op jit(solution)/shard_map/ppermute | solution.py:40
  22.2 7.6 %collective-permute-start.10 = (s16[4,88,128]{2,1,0:T(8,128)(2,1)S(1)}, s16[4,88,128]{2,1,0:T(8,128)(2,1)S(1)}, u32[]{:S(2)}, u32[]{:S(2)}) collective-permute-start(s16[4,88,128]{2,1,0:T(8,128)(2,1)S(1)} %pad_add_fusion), channel_id=1, source_target_pairs={{0,17},{1,16},{2,19},{3,18},{4,21},{5,20},{6,23},{7,22},{8,25},{9,... | collective-permute-start | bytes 270344 | tf_op jit(solution)/shard_map/ppermute | solution.py:46
  24.0 5.7 %collective-permute-start.9 = (s16[4,88,128]{2,1,0:T(8,128)(2,1)S(1)}, s16[4,88,128]{2,1,0:T(8,128)(2,1)S(1)}, u32[]{:S(2)}, u32[]{:S(2)}) collective-permute-start(s16[4,88,128]{2,1,0:T(8,128)(2,1)S(1)} %pad_add_fusion), channel_id=1, source_target_pairs={{0,16},{8,24},{16,0},{24,8},{1,17},{9,25},{17,1},{25,9},{2,18},{10... | collective-permute-start | bytes 270344 | tf_op jit(solution)/shard_map/ppermute | solution.py:40
  25.2 4.5 %collective-permute-start.8 = (s16[4,88,128]{2,1,0:T(8,128)(2,1)S(1)}, s16[4,88,128]{2,1,0:T(8,128)(2,1)S(1)}, u32[]{:S(2)}, u32[]{:S(2)}) collective-permute-start(s16[4,88,128]{2,1,0:T(8,128)(2,1)S(1)} %pad_add_fusion), channel_id=1, source_target_pairs={{0,1},{1,0},{2,3},{3,2},{4,5},{5,4},{6,7},{7,6},{8,9},{9,8},{10,11... | collective-permute-start | bytes 270344 | tf_op jit(solution)/shard_map/ppermute | solution.py:40
  29.8 1.7 %collective-permute-start.11 = (s16[16,88,128]{2,1,0:T(8,128)(2,1)S(1)}, s16[16,88,128]{2,1,0:T(8,128)(2,1)S(1)}, u32[]{:S(2)}, u32[]{:S(2)}) collective-permute-start(s16[16,88,128]{2,1,0:T(8,128)(2,1)S(1)} %constant_dynamic-update-slice_fusion.refs_0_), channel_id=1, source_target_pairs={{0,8},{8,0},{16,24},{24,16},{1,9},{9,1},{17,25},{25,17},{2,10},{10... | collective-permute-start | bytes 1081352 | tf_op jit(solution)/shard_map/ppermute | solution.py:40

commit v3 on v2

--- a/solution.py
+++ b/solution.py
@@ -111,7 +111,7 @@
 
 def sums_kernel(fields_ref, turned_ref, split_ref, part_ref, last_ref, acc_ref, tail_ref):
     count, levels, rows, cols = fields_ref.shape
-    matrix = count * 3 // 10
+    matrix = count * 7 // 20
     lead = lax.broadcasted_iota(jnp.int32, (8, rows), 1) - lax.broadcasted_iota(jnp.int32, (8, rows), 0)
     for level in range(levels):
         sums = [None] * count
@@ -293,13 +293,14 @@
     lon_size, lat_size = lax.axis_size("lon"), lax.axis_size("lat")
     count, levels, lat_rows, _ = fields.shape
     rows = count * levels
-    lon_bits = bits_of(lon_size)
     partner, counted = partner[None], counted[None]
 
     turned, split, shared = weights_of(area, ocean, counted)
     shared = shared[None]
-    for bit in lon_bits:
-        shared = jnp.concatenate([shared, exchange(shared, "lon", bit)], axis=0)
+    others = []
+    for mask in range(1, lon_size):
+        others.append(exchange(shared, "lon", mask))
+    shared = jnp.concatenate([shared] + others, axis=0)
     part, last = row_sums(fields, turned, split)
     pieces = add_fold(part, last, shared, partner, counted)
 

time: 32.7 us -> 32.5 us (level)
    ppermute x11 -> x12, starting transfers between devices: 11.6 us -> 11.3 us  [exchange(): return lax.ppermute(value, axis, [(i, i ^ bit) for i in range(size)])]
    ppermute x11 -> x12, waiting for transfers between devices: 12.9 us -> 12.9 us  [exchange(): return lax.ppermute(value, axis, [(i, i ^ bit) for i in range(size)])]
  transfers between devices with their start and end apart: 12 -> 13, of which waited for: 7 -> 7; matrix products, arithmetic and copies ran while one was open for 0% -> 0% of each run, Pallas kernels for 10% -> 10%
where the time goes in v3:
time: 32.5 us; the launch traced here: 32.3 us
  starting transfers between devices  13.2 us (41%)
  waiting for transfers between devices  12.9 us (40%)
  Pallas kernels  4.82 us (15%)
  local copies, waits for them, and re-layouts  1.32 us (4%)
    ppermute x12, waiting for transfers between devices, exchange(): return lax.ppermute(value, axis, [(i, i ^ bit) for i in range(size)])  12.9 us
    ppermute x12, starting transfers between devices, exchange(): return lax.ppermute(value, axis, [(i, i ^ bit) for i in range(size)])  11.3 us
    pallas_call x1, Pallas kernels, row_sums(): pl.pallas_call(sums_kernel, in_specs=[pl.BlockSpec(memory_space=VMEM)] *...  2.19 us
    pallas_call x2, Pallas kernels, place(): pl.pallas_call(functools.partial(place_kernel, masks, other), in_specs=sp...  1.96 us
    ppermute x1, starting transfers between devices, exchange_both(): return lax.ppermute(value, ('lon', 'lat'), pairs)  1.84 us
    unnamed x16, local copies, waits for them, and re-layouts  1.3 us
  transfers between devices with their start and end apart: 13, of which 7 were waited for; matrix products, arithmetic and copies ran while one was open for 0% of the time, Pallas kernels for 10%

profile of v3, /device:TPU:0, one launch (start us, length us, event | category | flops | bytes accessed | tf_op | source)
XLA Modules:
  0.0 32.3 jit_solution(12209068017191911629)
XLA Ops:
  0.0 0.7 %copy-done.3 = s32[512]{0:T(512)S(1)} copy-done((s32[512]{0:T(512)S(1)}, s32[512]{0:T(512)}, u32[]{:S(2)}) %copy-start.3) | copy-done | bytes 2072
  0.7 0.6 %copy-done.1 = s32[16,128,128]{2,1,0:T(8,128)S(1)} copy-done((s32[16,128,128]{2,1,0:T(8,128)S(1)}, s32[16,128,128]{2,1,0:T(8,128)}, u32[]{:S(2)}) %copy-start.1) | copy-done | bytes 1048600
  1.2 0.4 %cell_weights.1 = (f32[16,128,128]{2,1,0:T(8,128)S(1)}, bf16[16,256,128]{2,1,0:T(8,128)(2,1)S(1)}, f32[32,128]{1,0:T(8,128)S(1)}) custom-call(f32[8,128]{1,0:T(8,128)S(1)} %first.1._, f32[128,128]{1,0:T(8,128)S(1)} %copy-done.2, s32[16,128,128]{2,1,0:T(8,128)S(1)} %copy-done.1, s32[1,512]{1,0:T(1,128)S(1)} %bitcast.8), custom_call_target="tpu_custom_call" | custom-call | tf_op jit(solution)/shard_map/cell_weights/pallas_call | solution.py:94
  1.6 2.5 %collective-permute-start.2 = (f32[1,32,128]{2,1,0:T(8,128)S(1)}, f32[1,32,128]{2,1,0:T(8,128)S(1)}, u32[]{:S(2)}, u32[]{:S(2)}) collective-permute-start(f32[1,32,128]{2,1,0:T(8,128)S(1)} %bitcast.4), channel_id=1, source_target_pairs={{0,24},{8,16},{16,8},{24,0},{1,25},{9,17},{17,9},{25,1},{2,26},{10... | collective-permute-start | bytes 49160 | tf_op jit(solution)/shard_map/ppermute | solution.py:40
  4.1 0.6 %collective-permute-start.1 = (f32[1,32,128]{2,1,0:T(8,128)S(1)}, f32[1,32,128]{2,1,0:T(8,128)S(1)}, u32[]{:S(2)}, u32[]{:S(2)}) collective-permute-start(f32[1,32,128]{2,1,0:T(8,128)S(1)} %bitcast.5), channel_id=1, source_target_pairs={{0,16},{8,24},{16,0},{24,8},{1,17},{9,25},{17,1},{25,9},{2,18},{10... | collective-permute-start | bytes 49160 | tf_op jit(solution)/shard_map/ppermute | solution.py:40
  4.8 2.2 %row_sums.1 = (f32[320,128]{1,0:T(8,128)S(1)}, f32[320,128]{1,0:T(8,128)S(1)}) custom-call(bf16[20,16,128,128]{3,2,1,0:T(8,128)(2,1)S(1)} %copy-done, f32[16,128,128]{2,1,0:T(8,128)S(1)} %get-tuple-element.15.turned_ref, bf16[16,256,128]{2,1,0:T(8,128)(2,1)S(1)} %get-tuple-element.16.split_ref), custom_call_target="tpu_custom_call" | custom-call | tf_op jit(solution)/shard_map/row_sums/pallas_call | solution.py:144
  7.0 0.9 %collective-permute-done.1 = f32[1,32,128]{2,1,0:T(8,128)S(1)} collective-permute-done((f32[1,32,128]{2,1,0:T(8,128)S(1)}, f32[1,32,128]{2,1,0:T(8,128)S(1)}, u32[]{:S(2)}, u32[]{:S(2)}) %collective-permute-start.1) | collective-permute-done | bytes 16416 | tf_op jit(solution)/shard_map/ppermute | solution.py:40
  7.9 0.2 add_fold.1
  8.1 0.1 collective-permute-start.3
  8.2 1.8 %collective-permute-start.4 = (f32[80,128]{1,0:T(8,128)S(1)}, f32[80,128]{1,0:T(8,128)S(1)}, u32[]{:S(2)}, u32[]{:S(2)}) collective-permute-start(f32[80,128]{1,0:T(8,128)S(1)} %get-tuple-element.21), channel_id=1, source_target_pairs={{0,16},{8,24},{16,0},{24,8},{1,17},{9,25},{17,1},{25,9},{2,18},{10... | collective-permute-start | bytes 122888 | tf_op jit(solution)/shard_map/ppermute | solution.py:40
  10.0 0.1 collective-permute-start.5
  10.0 2.2 %collective-permute-done.4.refs_2_ = f32[80,128]{1,0:T(8,128)S(1)} collective-permute-done((f32[80,128]{1,0:T(8,128)S(1)}, f32[80,128]{1,0:T(8,128)S(1)}, u32[]{:S(2)}, u32[]{:S(2)}) %collective-permute-start.4) | collective-permute-done | bytes 40992 | tf_op jit(solution)/shard_map/ppermute | solution.py:40
  12.3 1.2 %collective-permute-done.5.refs_3_ = f32[80,128]{1,0:T(8,128)S(1)} collective-permute-done((f32[80,128]{1,0:T(8,128)S(1)}, f32[80,128]{1,0:T(8,128)S(1)}, u32[]{:S(2)}, u32[]{:S(2)}) %collective-permute-start.5) | collective-permute-done | bytes 40992 | tf_op jit(solution)/shard_map/ppermute | solution.py:40
  13.6 3.7 %collective-permute-start.8 = (s16[1,88,128]{2,1,0:T(8,128)(2,1)S(1)}, s16[1,88,128]{2,1,0:T(8,128)(2,1)S(1)}, u32[]{:S(2)}, u32[]{:S(2)}) collective-permute-start(s16[1,88,128]{2,1,0:T(8,128)(2,1)S(1)} %finish.1), channel_id=1, source_target_pairs={{0,6},{1,7},{2,4},{3,5},{4,2},{5,3},{6,0},{7,1},{8,14},{9,15},{10,... | collective-permute-start | bytes 67592 | tf_op jit(solution)/shard_map/ppermute | solution.py:40
  17.2 0.8 %collective-permute-start.6 = (s16[1,88,128]{2,1,0:T(8,128)(2,1)S(1)}, s16[1,88,128]{2,1,0:T(8,128)(2,1)S(1)}, u32[]{:S(2)}, u32[]{:S(2)}) collective-permute-start(s16[1,88,128]{2,1,0:T(8,128)(2,1)S(1)} %finish.1), channel_id=1, source_target_pairs={{0,2},{1,3},{2,0},{3,1},{4,6},{5,7},{6,4},{7,5},{8,10},{9,11},{10,... | collective-permute-start | bytes 67592 | tf_op jit(solution)/shard_map/ppermute | solution.py:40
  18.0 1.2 %collective-permute-done.8 = s16[1,88,128]{2,1,0:T(8,128)(2,1)S(1)} collective-permute-done((s16[1,88,128]{2,1,0:T(8,128)(2,1)S(1)}, s16[1,88,128]{2,1,0:T(8,128)(2,1)S(1)}, u32[]{:S(2)}, u32[]{:S(2)}) %collective-permute-start.8) | collective-permute-done | bytes 22560 | tf_op jit(solution)/shard_map/ppermute | solution.py:40
  19.2 2.7 %collective-permute-done.7 = s16[1,88,128]{2,1,0:T(8,128)(2,1)S(1)} collective-permute-done((s16[1,88,128]{2,1,0:T(8,128)(2,1)S(1)}, s16[1,88,128]{2,1,0:T(8,128)(2,1)S(1)}, u32[]{:S(2)}, u32[]{:S(2)}) %collective-permute-start.7) | collective-permute-done | bytes 22560 | tf_op jit(solution)/shard_map/ppermute | solution.py:40
  22.0 1.8 %collective-permute-start.11 = (s16[4,88,128]{2,1,0:T(8,128)(2,1)S(1)}, s16[4,88,128]{2,1,0:T(8,128)(2,1)S(1)}, u32[]{:S(2)}, u32[]{:S(2)}) collective-permute-start(s16[4,88,128]{2,1,0:T(8,128)(2,1)S(1)} %pad_add_fusion), channel_id=1, source_target_pairs={{0,17},{1,16},{2,19},{3,18},{4,21},{5,20},{6,23},{7,22},{8,25},{9,... | collective-permute-start | bytes 270344 | tf_op jit(solution)/shard_map/ppermute | solution.py:46
  23.8 1.2 %collective-permute-start.10 = (s16[4,88,128]{2,1,0:T(8,128)(2,1)S(1)}, s16[4,88,128]{2,1,0:T(8,128)(2,1)S(1)}, u32[]{:S(2)}, u32[]{:S(2)}) collective-permute-start(s16[4,88,128]{2,1,0:T(8,128)(2,1)S(1)} %pad_add_fusion), channel_id=1, source_target_pairs={{0,16},{8,24},{16,0},{24,8},{1,17},{9,25},{17,1},{25,9},{2,18},{10... | collective-permute-start | bytes 270344 | tf_op jit(solution)/shard_map/ppermute | solution.py:40
  25.0 0.5 %collective-permute-start.9 = (s16[4,88,128]{2,1,0:T(8,128)(2,1)S(1)}, s16[4,88,128]{2,1,0:T(8,128)(2,1)S(1)}, u32[]{:S(2)}, u32[]{:S(2)}) collective-permute-start(s16[4,88,128]{2,1,0:T(8,128)(2,1)S(1)} %pad_add_fusion), channel_id=1, source_target_pairs={{0,1},{1,0},{2,3},{3,2},{4,5},{5,4},{6,7},{7,6},{8,9},{9,8},{10,11... | collective-permute-start | bytes 270344 | tf_op jit(solution)/shard_map/ppermute | solution.py:40
  25.5 4.0 %collective-permute-done.9 = s16[4,88,128]{2,1,0:T(8,128)(2,1)S(1)} collective-permute-done((s16[4,88,128]{2,1,0:T(8,128)(2,1)S(1)}, s16[4,88,128]{2,1,0:T(8,128)(2,1)S(1)}, u32[]{:S(2)}, u32[]{:S(2)}) %collective-permute-start.9) | collective-permute-done | bytes 90144 | tf_op jit(solution)/shard_map/ppermute | solution.py:40
  29.7 1.0 %shard_map.55.refs_1_ = f32[320,1024]{1,0:T(8,128)} custom-call(s16[16,88,128]{2,1,0:T(8,128)(2,1)S(1)} %constant_dynamic-update-slice_fusion.refs_0_), custom_call_target="tpu_custom_call" | custom-call | tf_op jit(solution)/shard_map/pallas_call | solution.py:278
  30.7 0.7 %collective-permute-done.12.refs_0_ = s16[16,88,128]{2,1,0:T(8,128)(2,1)S(1)} collective-permute-done((s16[16,88,128]{2,1,0:T(8,128)(2,1)S(1)}, s16[16,88,128]{2,1,0:T(8,128)(2,1)S(1)}, u32[]{:S(2)}, u32[]{:S(2)}) %collective-permute-start.12) | collective-permute-done | bytes 360480 | tf_op jit(solution)/shard_map/ppermute | solution.py:40
  31.3 1.0 %shard_map.56 = f32[320,1024]{1,0:T(8,128)} custom-call(s16[16,88,128]{2,1,0:T(8,128)(2,1)S(1)} %collective-permute-done.12.refs_0_, f32[320,1024]{1,0:T(8,128)} %shard_map.55.refs_1_), custom_call_target="tpu_custom_call", output_to_operand_aliasing={{}: (1, {})} | custom-call | tf_op jit(solution)/shard_map/pallas_call | solution.py:278
  (28 shorter events, 0.3 us)
Async XLA Ops:
  0.0 0.7 %copy-start.3 = (s32[512]{0:T(512)S(1)}, s32[512]{0:T(512)}, u32[]{:S(2)}) copy-start(s32[512]{0:T(512)} %param.9) | copy-start | bytes 6148
  0.0 1.2 %copy-start.1 = (s32[16,128,128]{2,1,0:T(8,128)S(1)}, s32[16,128,128]{2,1,0:T(8,128)}, u32[]{:S(2)}) copy-start(s32[16,128,128]{2,1,0:T(8,128)} %ocean_ref.1) | copy-start | bytes 3145732
  0.0 1.2 %copy-start.2 = (f32[128,128]{1,0:T(8,128)S(1)}, f32[128,128]{1,0:T(8,128)}, u32[]{:S(2)}) copy-start(f32[128,128]{1,0:T(8,128)} %area_ref.1) | copy-start | bytes 196612
  0.0 4.8 %copy-start = (bf16[20,16,128,128]{3,2,1,0:T(8,128)(2,1)S(1)}, bf16[20,16,128,128]{3,2,1,0:T(8,128)(2,1)}, u32[]{:S(2)}) copy-start(bf16[20,16,128,128]{3,2,1,0:T(8,128)(2,1)} %fields_ref.1) | copy-start | bytes 31457284
  1.6 5.4 %collective-permute-start.2 = (f32[1,32,128]{2,1,0:T(8,128)S(1)}, f32[1,32,128]{2,1,0:T(8,128)S(1)}, u32[]{:S(2)}, u32[]{:S(2)}) collective-permute-start(f32[1,32,128]{2,1,0:T(8,128)S(1)} %bitcast.4), channel_id=1, source_target_pairs={{0,24},{8,16},{16,8},{24,0},{1,25},{9,17},{17,9},{25,1},{2,26},{10... | collective-permute-start | bytes 49160 | tf_op jit(solution)/shard_map/ppermute | solution.py:40
  4.1 3.7 %collective-permute-start.1 = (f32[1,32,128]{2,1,0:T(8,128)S(1)}, f32[1,32,128]{2,1,0:T(8,128)S(1)}, u32[]{:S(2)}, u32[]{:S(2)}) collective-permute-start(f32[1,32,128]{2,1,0:T(8,128)S(1)} %bitcast.5), channel_id=1, source_target_pairs={{0,16},{8,24},{16,0},{24,8},{1,17},{9,25},{17,1},{25,9},{2,18},{10... | collective-permute-start | bytes 49160 | tf_op jit(solution)/shard_map/ppermute | solution.py:40
  4.8 3.1 %collective-permute-start = (f32[1,32,128]{2,1,0:T(8,128)S(1)}, f32[1,32,128]{2,1,0:T(8,128)S(1)}, u32[]{:S(2)}, u32[]{:S(2)}) collective-permute-start(f32[1,32,128]{2,1,0:T(8,128)S(1)} %bitcast.6), channel_id=1, source_target_pairs={{0,8},{8,0},{16,24},{24,16},{1,9},{9,1},{17,25},{25,17},{2,10},{10... | collective-permute-start | bytes 49160 | tf_op jit(solution)/shard_map/ppermute | solution.py:40
  4.8 3.1 %copy-start.4 = (s32[512]{0:T(512)S(1)}, s32[512]{0:T(512)}, u32[]{:S(2)}) copy-start(s32[512]{0:T(512)} %param.8) | copy-start | bytes 6148
  8.1 1.9 %collective-permute-start.3 = (f32[80,128]{1,0:T(8,128)S(1)}, f32[80,128]{1,0:T(8,128)S(1)}, u32[]{:S(2)}, u32[]{:S(2)}) collective-permute-start(f32[80,128]{1,0:T(8,128)S(1)} %get-tuple-element.20), channel_id=1, source_target_pairs={{0,8},{8,0},{16,24},{24,16},{1,9},{9,1},{17,25},{25,17},{2,10},{10... | collective-permute-start | bytes 122888 | tf_op jit(solution)/shard_map/ppermute | solution.py:40
  8.2 4.1 %collective-permute-start.4 = (f32[80,128]{1,0:T(8,128)S(1)}, f32[80,128]{1,0:T(8,128)S(1)}, u32[]{:S(2)}, u32[]{:S(2)}) collective-permute-start(f32[80,128]{1,0:T(8,128)S(1)} %get-tuple-element.21), channel_id=1, source_target_pairs={{0,16},{8,24},{16,0},{24,8},{1,17},{9,25},{17,1},{25,9},{2,18},{10... | collective-permute-start | bytes 122888 | tf_op jit(solution)/shard_map/ppermute | solution.py:40
  10.0 3.5 %collective-permute-start.5 = (f32[80,128]{1,0:T(8,128)S(1)}, f32[80,128]{1,0:T(8,128)S(1)}, u32[]{:S(2)}, u32[]{:S(2)}) collective-permute-start(f32[80,128]{1,0:T(8,128)S(1)} %get-tuple-element.22), channel_id=1, source_target_pairs={{0,24},{8,16},{16,8},{24,0},{1,25},{9,17},{17,9},{25,1},{2,26},{10... | collective-permute-start | bytes 122888 | tf_op jit(solution)/shard_map/ppermute | solution.py:40
  13.6 5.7 %collective-permute-start.8 = (s16[1,88,128]{2,1,0:T(8,128)(2,1)S(1)}, s16[1,88,128]{2,1,0:T(8,128)(2,1)S(1)}, u32[]{:S(2)}, u32[]{:S(2)}) collective-permute-start(s16[1,88,128]{2,1,0:T(8,128)(2,1)S(1)} %finish.1), channel_id=1, source_target_pairs={{0,6},{1,7},{2,4},{3,5},{4,2},{5,3},{6,0},{7,1},{8,14},{9,15},{10,... | collective-permute-start | bytes 67592 | tf_op jit(solution)/shard_map/ppermute | solution.py:40
  17.2 4.7 %collective-permute-start.7 = (s16[1,88,128]{2,1,0:T(8,128)(2,1)S(1)}, s16[1,88,128]{2,1,0:T(8,128)(2,1)S(1)}, u32[]{:S(2)}, u32[]{:S(2)}) collective-permute-start(s16[1,88,128]{2,1,0:T(8,128)(2,1)S(1)} %finish.1), channel_id=1, source_target_pairs={{0,4},{1,5},{2,6},{3,7},{4,0},{5,1},{6,2},{7,3},{8,12},{9,13},{10,... | collective-permute-start | bytes 67592 | tf_op jit(solution)/shard_map/ppermute | solution.py:40
  17.2 4.7 %collective-permute-start.6 = (s16[1,88,128]{2,1,0:T(8,128)(2,1)S(1)}, s16[1,88,128]{2,1,0:T(8,128)(2,1)S(1)}, u32[]{:S(2)}, u32[]{:S(2)}) collective-permute-start(s16[1,88,128]{2,1,0:T(8,128)(2,1)S(1)} %finish.1), channel_id=1, source_target_pairs={{0,2},{1,3},{2,0},{3,1},{4,6},{5,7},{6,4},{7,5},{8,10},{9,11},{10,... | collective-permute-start | bytes 67592 | tf_op jit(solution)/shard_map/ppermute | solution.py:40
  22.0 7.6 %collective-permute-start.11 = (s16[4,88,128]{2,1,0:T(8,128)(2,1)S(1)}, s16[4,88,128]{2,1,0:T(8,128)(2,1)S(1)}, u32[]{:S(2)}, u32[]{:S(2)}) collective-permute-start(s16[4,88,128]{2,1,0:T(8,128)(2,1)S(1)} %pad_add_fusion), channel_id=1, source_target_pairs={{0,17},{1,16},{2,19},{3,18},{4,21},{5,20},{6,23},{7,22},{8,25},{9,... | collective-permute-start | bytes 270344 | tf_op jit(solution)/shard_map/ppermute | solution.py:46
  23.8 5.7 %collective-permute-start.10 = (s16[4,88,128]{2,1,0:T(8,128)(2,1)S(1)}, s16[4,88,128]{2,1,0:T(8,128)(2,1)S(1)}, u32[]{:S(2)}, u32[]{:S(2)}) collective-permute-start(s16[4,88,128]{2,1,0:T(8,128)(2,1)S(1)} %pad_add_fusion), channel_id=1, source_target_pairs={{0,16},{8,24},{16,0},{24,8},{1,17},{9,25},{17,1},{25,9},{2,18},{10... | collective-permute-start | bytes 270344 | tf_op jit(solution)/shard_map/ppermute | solution.py:40
  25.0 4.5 %collective-permute-start.9 = (s16[4,88,128]{2,1,0:T(8,128)(2,1)S(1)}, s16[4,88,128]{2,1,0:T(8,128)(2,1)S(1)}, u32[]{:S(2)}, u32[]{:S(2)}) collective-permute-start(s16[4,88,128]{2,1,0:T(8,128)(2,1)S(1)} %pad_add_fusion), channel_id=1, source_target_pairs={{0,1},{1,0},{2,3},{3,2},{4,5},{5,4},{6,7},{7,6},{8,9},{9,8},{10,11... | collective-permute-start | bytes 270344 | tf_op jit(solution)/shard_map/ppermute | solution.py:40
  29.6 1.7 %collective-permute-start.12 = (s16[16,88,128]{2,1,0:T(8,128)(2,1)S(1)}, s16[16,88,128]{2,1,0:T(8,128)(2,1)S(1)}, u32[]{:S(2)}, u32[]{:S(2)}) collective-permute-start(s16[16,88,128]{2,1,0:T(8,128)(2,1)S(1)} %constant_dynamic-update-slice_fusion.refs_0_), channel_id=1, source_target_pairs={{0,8},{8,0},{16,24},{24,16},{1,9},{9,1},{17,25},{25,17},{2,10},{10... | collective-permute-start | bytes 1081352 | tf_op jit(solution)/shard_map/ppermute | solution.py:40
